TPU v7x, 16 devices: a whole 2x2x2 slice. The times are simulated.
16 devices in a mesh: col: 4 (over z, y), row: 4 (over x, core).
Axes of the slice: x: 2, y: 2, z: 2, core: 2. Of those that a mesh axis runs over, the one named last changes fastest.
Arguments:
- vel_x: float32 [60, 2, 128, 1024], P(None, None, 'row', 'col')
- vel_y: float32 [60, 2, 128, 1024], P(None, None, 'row', 'col')
- pot_temp: float32 [60, 2, 128, 1024], P(None, None, 'row', 'col')
- salinity: float32 [60, 2, 128, 1024], P(None, None, 'row', 'col')
- surf_eta: float32 [2, 128, 1024], P(None, 'row', 'col')
- trans_x: float32 [2, 128, 1024], P(None, 'row', 'col')
- trans_y: float32 [2, 128, 1024], P(None, 'row', 'col')
- col_depth: float32 [128, 1024], P('row', 'col')
- wet_levels: int32 [128, 1024], P('row', 'col')
- avg_weights: float32 [40], replicated
Outputs:
- output 1: float32 [2, 128, 1024], P(None, 'row', 'col')
- output 2: float32 [2, 128, 1024], P(None, 'row', 'col')
- output 3: float32 [2, 128, 1024], P(None, 'row', 'col')
- output 4: float32 [60, 2, 128, 1024], P(None, None, 'row', 'col')
- output 5: float32 [60, 2, 128, 1024], P(None, None, 'row', 'col')
- output 6: float32 [60, 2, 128, 1024], P(None, None, 'row', 'col')
- output 7: float32 [60, 2, 128, 1024], P(None, None, 'row', 'col')
All inputs are finite; a program needn't handle non-finite values.
Results may differ from a plain program's by a relative error of at most 0.001.
Values sent between devices are 32-bit elements.
A program may use at most 1 GiB of HBM per device.

v0:
```python
import functools
import jax
import jax.numpy as jnp
import numpy as np
from jax import lax
from jax.experimental import pallas as pl
from jax.experimental.pallas import tpu as pltpu
from jax.sharding import PartitionSpec as P

MESH = pl.DeviceIdType.MESH
F32 = jnp.float32
NK = 60
NM = 2
NY = 32
NL = 128
NS = 8
VR = (NS, NL)
NX = 256
NT = NX // NL
NJ = NY // 8
CH = 10
NC = NK // CH
HALO = 40
WY = 2 * NY + HALO
WJ = WY // 8
WT = 3
NSUB = 40
COURANT = 0.4
VMEM_LIMIT = 42 << 20
SIDE = 40

VM = pl.BlockSpec(memory_space=pltpu.VMEM)
SM = pl.BlockSpec(memory_space=pltpu.SMEM)
ANY = pl.BlockSpec(memory_space=pl.ANY)


def level_table():
    rows = np.zeros((4, NK), np.float64)
    for row, strength in ((0, 1.0), (2, 0.5)):
        scale = 1.0 if strength == 1.0 else 0.5
        div_prev = 0.0
        for k in range(NK):
            if k == 0:
                div = 1.0 + strength
            else:
                div = 1.0 + 2.0 * strength - strength * strength / div_prev
            rows[row, k] = scale / div
            rows[row + 1, k] = scale / (div - strength)
            div_prev = div
    return jnp.asarray(rows, F32)


def lanes_iota():
    return lax.broadcasted_iota(jnp.int32, VR, 1)


def subl_iota():
    return lax.broadcasted_iota(jnp.int32, VR, 0)


def device(col, row):
    return {"col": col, "row": row}


def greet(col, row):
    barrier = pltpu.get_barrier_semaphore()
    count = 0
    for dc in (0, 1, 3):
        for dr in range(4):
            if dc == 0 and dr == 0:
                continue
            pl.semaphore_signal(barrier, inc=1, device_id=device(lax.rem(col + dc, 4), lax.rem(row + dr, 4)), device_id_type=MESH)
            count += 1
    pl.semaphore_wait(barrier, count)


class Exchange:
    def __init__(self, src_main, src_side, main, side, send_sem, recv_sem, col, row):
        chip = row // 2
        core = lax.rem(row, 2)
        east = lax.rem(col + 1, 4)
        west = lax.rem(col + 3, 4)
        self.full = chip != core
        self.main, self.side, self.recv_sem = main, side, recv_sem
        own = pl.ds(pl.multiple_of(core * NY, NS), NY)
        at_full = pl.ds(pl.multiple_of(jnp.where(chip == 1, 2 * NY, NY + HALO), NS), NY)
        at_part = pl.ds(pl.multiple_of(jnp.where(chip == 1, 3 * NY, 2 * NY), NS), NS)
        from_part = pl.ds(pl.multiple_of(jnp.where(chip == 1, 0, NY - NS), NS), NS)
        self.count = 0

        def remote(s, d, kind, dev):
            return pltpu.make_async_remote_copy(src_ref=s, dst_ref=d, send_sem=send_sem.at[self.count], recv_sem=recv_sem.at[kind], device_id=dev, device_id_type=MESH)

        self.always, self.whole, self.part = [], [], []
        self.local = pltpu.make_async_copy(src_main.at[core], main.at[:, :, own], recv_sem.at[0])
        self.always.append(remote(src_main.at[1 - core], main.at[:, :, own], 0, device(col, chip * 2 + 1 - core)))
        for mm in range(NM):
            near, far = chip * 2 + mm, (1 - chip) * 2 + mm
            self.count += 1
            self.whole.append(remote(src_main.at[mm], main.at[:, :, at_full], 0, device(col, far)))
            self.part.append(remote(src_main.at[mm, :, :, from_part], main.at[:, :, at_part], 0, device(col, far)))
            for e, dev in enumerate((west, east)):
                self.count += 1
                self.whole.append(remote(src_side.at[mm, e], side.at[e, :, at_full], 1, device(dev, far)))
                self.part.append(remote(src_side.at[mm, e, :, from_part], side.at[e, :, at_part], 1, device(dev, far)))
                self.count += 1
                self.always.append(remote(src_side.at[mm, e], side.at[e, :, own], 1, device(dev, near)))

    def branch(self, op):
        @pl.when(self.full)
        def _():
            for copy in self.whole:
                getattr(copy, op)()

        @pl.when(jnp.logical_not(self.full))
        def _():
            for copy in self.part:
                getattr(copy, op)()

    def start(self):
        self.branch("start")
        for copy in self.always:
            copy.start()
        self.local.start()

    def wait(self):
        pltpu.make_async_copy(self.main, self.main, self.recv_sem.at[0]).wait()
        pltpu.make_async_copy(self.side, self.side, self.recv_sem.at[1]).wait()
        for copy in self.always:
            copy.wait_send()
        self.branch("wait_send")


def pack_side(dst, m, group, fields, lane):
    for i in range(NY // NS):
        rows = pl.ds(i * NS, NS)
        first = fields[0](0, rows)
        last = fields[0](NT - 1, rows)
        for n in range(1, len(fields)):
            first = jnp.where(lane < n * SIDE, first, pltpu.roll(fields[n](0, rows), n * SIDE, 1))
            last = jnp.where(lane >= NL - n * SIDE, last, pltpu.roll(fields[n](NT - 1, rows), NL - n * SIDE, 1))
        dst[m, 0, group, rows] = first
        dst[m, 1, group, rows] = last


def window_tile(main, side, f, j, t, lane, group, place):
    here = pl.ds(j, NS, stride=WJ)
    if t < NT:
        return main.at[f, t][here, :]
    e, w = side.at[0, group][here, :], side.at[1, group][here, :]
    if place:
        e, w = pltpu.roll(e, NL - place * SIDE, 1), pltpu.roll(w, place * SIDE, 1)
    return jnp.where(lane < SIDE, e, jnp.where(lane >= NL - SIDE, w, 0.0))


PA = 0.15 * 0.5 / NK * 0.5
PB = 0.2 * 0.5 / NK * 0.5
MOM_UNROLL = 1
TRC_UNROLL = 3


def step_kernel(u, v, temp, salt, eta, tx, ty, depth, wet, weights, tab,
                sbuf, bsum, kl, rl, out,
                inb, hE, hW, hN, hS, hSE, hNW, colF, colL, rowF, rowL, ksrc, kE, kN,
                wmain, wside, main, side, gsum, fmain, fside, fwin, fwside, wi, nat, state, res,
                in_sem, sendC, recvE, recvW, sendR, recvN, recvS, corn_send, corn_recv, k_send, k_recv,
                w_send, w_recv, f_send, f_recv, out_send, out_recv, loc_sem):
    col = lax.axis_index("col")
    row = lax.axis_index("row")
    chip = row // 2
    core = lax.rem(row, 2)
    east_dev = lax.rem(col + 1, 4)
    west_dev = lax.rem(col + 3, 4)
    north_dev = jnp.minimum(row + 1, 3)
    south_dev = jnp.maximum(row - 1, 0)
    has_north = row < 3
    has_south = row > 0
    fields = (u, v, temp, salt)
    lane = lanes_iota()
    subl = subl_iota()
    l_last, l_first = lane == NL - 1, lane == 0
    s_last, s_first = subl == NS - 1, subl == 0
    zero = jnp.zeros(VR, F32)

    def load(f, m, t, c):
        part = pl.ds(c * CH, CH)
        return pltpu.make_async_copy(fields[f].at[part, m, :, pl.ds(t * NL, NL)], inb.at[f, m, t, part], in_sem.at[f, m, t, c])

    def each_load(f, c, op):
        for m in range(NM):
            for t in range(NT):
                getattr(load(f, m, t, c), op)()

    for f in range(4):
        for c in range(NC):
            each_load(f, c, "start")

    for t in range(NT):
        ksrc[t] = wet[:, pl.ds(t * NL, NL)].astype(F32)

    greet(col, row)

    def remote(s, d, ssem, rsem, dc, dr):
        return pltpu.make_async_remote_copy(src_ref=s, dst_ref=d, send_sem=ssem, recv_sem=rsem, device_id=device(dc, dr), device_id_type=MESH)

    k_west = remote(ksrc.at[0], kE, k_send.at[0], k_recv.at[0], west_dev, row)
    k_south = remote(ksrc.at[:, pl.ds(0, NS)], kN, k_send.at[1], k_recv.at[1], col, south_dev)

    def col_copies(f):
        return (remote(colF.at[f], hE.at[f], sendC.at[0, f], recvE.at[f], west_dev, row),
                remote(colL.at[f], hW.at[f], sendC.at[1, f], recvW.at[f], east_dev, row))

    def to_south(f):
        return remote(rowF.at[f], hN.at[f], sendR.at[0, f], recvN.at[f], col, south_dev)

    def to_north(f):
        return remote(rowL.at[f], hS.at[f], sendR.at[1, f], recvS.at[f], col, north_dev)

    corner_north = remote(colF.at[1, pl.ds(NY - NS, NS)], hSE, corn_send.at[0], corn_recv.at[0], west_dev, north_dev)
    corner_south = remote(colL.at[0, pl.ds(0, NS)], hNW, corn_send.at[1], corn_recv.at[1], east_dev, south_dev)

    k_west.start()

    @pl.when(has_south)
    def _():
        k_south.start()

    half_lane = NL // 2
    for f in range(4):
        def chunk(c, acc, f=f):
            each_load(f, c, "wait")
            acc = list(acc)
            for q in range(CH):
                k = c * CH + q
                for m in range(NM):
                    spot = k + half_lane * m
                    hit = lane == spot
                    for i in range(NJ):
                        rows = pl.ds(i * NS, NS)
                        first = pltpu.roll(inb[f, m, 0, k, rows], spot, 1)
                        last = pltpu.roll(inb[f, m, NT - 1, k, rows], lax.rem(spot + 1, NL), 1)
                        acc[2 * i] = jnp.where(hit, first, acc[2 * i])
                        acc[2 * i + 1] = jnp.where(hit, last, acc[2 * i + 1])
                    for t in range(NT):
                        rowF[f, t, pl.ds(m * NK + k, 1), :] = inb[f, m, t, k, 0:1]
                        rowL[f, t, pl.ds(m * NK + k, 1), :] = inb[f, m, t, k, NY - 1:NY]
            return tuple(acc)

        acc = lax.fori_loop(0, NC, chunk, (zero,) * (2 * NJ))
        for i in range(NJ):
            colF[f, pl.ds(i * NS, NS)] = acc[2 * i]
            colL[f, pl.ds(i * NS, NS)] = acc[2 * i + 1]

        @pl.when(has_south)
        def _():
            to_south(f).start()

        @pl.when(has_north)
        def _():
            to_north(f).start()
        for copy in col_copies(f):
            copy.start()
        if f == 0:
            @pl.when(has_south)
            def _():
                corner_south.start()
        if f == 1:
            @pl.when(has_north)
            def _():
                corner_north.start()

    for m in range(NM):
        for t in range(NT):
            cols = pl.ds(t * NL, NL)
            for i, arr in enumerate((eta, tx, ty)):
                wmain[m, i, t] = arr[m, :, cols]
            wmain[m, 3, t] = depth[:, cols]
            wmain[m, 4, t] = ksrc[t]
        reads = [lambda t, rows, m=m, i=i: wmain[m, i, t, rows] for i in range(5)]
        pack_side(wside, m, 0, reads[:3], lane)
        pack_side(wside, m, 1, reads[3:], lane)
    windows = Exchange(wmain, wside, main, side, w_send, w_recv, col, row)
    windows.start()

    @pl.when(jnp.logical_not(has_north))
    def _():
        hN[...] = jnp.zeros(hN.shape, F32)
        hNW[...] = jnp.zeros(hNW.shape, F32)
        kN[...] = jnp.zeros(kN.shape, F32)

    @pl.when(jnp.logical_not(has_south))
    def _():
        hS[...] = jnp.zeros(hS.shape, F32)
        hSE[...] = jnp.zeros(hSE.shape, F32)

    for f in range(4):
        for m in range(NM):
            for i in range(NJ * NT):
                sbuf[f, m, 0, i] = zero
    for f in range(2):
        for m in range(NM):
            for i in range(NJ * NT):
                gsum[f, m, i] = zero
                bsum[f, m, i] = zero

    k_west.wait()

    @pl.when(has_south)
    def _():
        k_south.wait_send()
        corner_south.wait_send()
        corner_north.wait_recv()

    @pl.when(has_north)
    def _():
        k_south.wait_recv()
        corner_north.wait_send()
        corner_south.wait_recv()

    for f in range(4):
        for copy in col_copies(f):
            copy.wait()

        @pl.when(has_south)
        def _():
            to_south(f).wait_send()
            to_north(f).wait_recv()

        @pl.when(has_north)
        def _():
            to_north(f).wait_send()
            to_south(f).wait_recv()

    def rolls(x, amount):
        return [[pltpu.roll(x[j][t], amount, 1) for t in range(NT)] for j in range(NJ)]

    def east(x, halo):
        r = rolls(x, NL - 1)
        return [[jnp.where(l_last, r[j][1] if t == 0 else halo[j], r[j][t]) for t in range(NT)] for j in range(NJ)]

    def west(x, halo):
        r = rolls(x, 1)
        return [[jnp.where(l_first, r[j][0] if t == 1 else halo[j], r[j][t]) for t in range(NT)] for j in range(NJ)]

    def north(x, halo):
        return x[1:] + [[jnp.where(s_last, halo[t], pltpu.roll(x[0][t], NS - 1, 0)) for t in range(NT)]]

    def south(x, halo):
        return [[jnp.where(s_first, halo[t], pltpu.roll(x[NJ - 1][t], 1, 0)) for t in range(NT)]] + x[:-1]

    def zipped(fn, *xs):
        return [[fn(*[x[j][t] for x in xs]) for t in range(NT)] for j in range(NJ)]

    def strided(ref):
        return [ref[pl.ds(j, NS, stride=NJ), :] for j in range(NJ)]

    k_mid = zipped(lambda x: x, [list(pair) for pair in zip(*[strided(ksrc.at[t]) for t in range(NT)])])
    k_east = zipped(jnp.minimum, k_mid, east(k_mid, [pltpu.roll(x, NL - 1, 1) for x in strided(kE)]))
    k_north = zipped(jnp.minimum, k_mid, north(k_mid, [kN.at[t][pl.ds(0, NS, stride=0), :] for t in range(NT)]))
    for n, mask in enumerate((k_mid, k_east, k_north)):
        for j in range(NJ):
            for t in range(NT):
                kl[n, j * NT + t] = mask[j][t].astype(jnp.int32)

    def read_mask(n):
        return [[kl[n, j * NT + t] for t in range(NT)] for j in range(NJ)]

    def factors(mask, k, a, b):
        return zipped(lambda n: jnp.where(n > k + 1, a, jnp.where(n == k + 1, b, 0.0)), mask)

    def block(f, m, k):
        return [[inb.at[f, m, t, k][pl.ds(j, NS, stride=NJ), :] for t in range(NT)] for j in range(NJ)]

    def line(ref, f, m, k):
        return [ref.at[f, t][pl.ds(m * NK + k, NS, stride=0), :] for t in range(NT)]

    def amounts(m, k):
        return NL - 1 - half_lane * m - k, lax.rem(NL - half_lane * m - k, NL)

    def edge(ref, f, amount):
        return [pltpu.roll(x, amount, 1) for x in strided(ref.at[f])]

    def solve(f, m, k, side_k, scale):
        for j in range(NJ):
            for t in range(NT):
                i = j * NT + t
                sbuf[f, m, k + 1, i] = (side_k[j][t] + sbuf[f, m, k, i]) * scale[j][t]

    def momentum(m, k, carry, wet_x, wet_y, inv_x, inv_y):
        cs, cs_n, cs_e = carry
        uu, vv, tt, ss = (block(f, m, k) for f in range(4))
        to_last, to_first = amounts(m, k)
        eu, ev, et, es = (edge(hE, f, to_last) for f in range(4))
        wu, wv = (edge(hW, f, to_first) for f in range(2))
        nu, nv, nt, ns = (line(hN, f, m, k) for f in range(4))
        su, sv = (line(hS, f, m, k) for f in range(2))
        c_se = pltpu.roll(hSE[pl.ds(NS - 1, NS, stride=0), :], to_last, 1)
        c_nw = pltpu.roll(hNW[pl.ds(0, NS, stride=0), :], to_first, 1)

        half = zipped(lambda s, t: PA * s - PB * t, ss, tt)
        p = zipped(jnp.add, cs, half)
        cs = zipped(jnp.add, p, half)
        half_n = [PA * ns[t] - PB * nt[t] for t in range(NT)]
        p_n = [cs_n[t] + half_n[t] for t in range(NT)]
        cs_n = [p_n[t] + half_n[t] for t in range(NT)]
        half_e = [PA * es[j] - PB * et[j] for j in range(NJ)]
        p_e = [cs_e[j] + half_e[j] for j in range(NJ)]
        cs_e = [p_e[j] + half_e[j] for j in range(NJ)]

        u_e, u_w, v_e, v_w = east(uu, eu), west(uu, wu), east(vv, ev), west(vv, wv)
        u_n, u_s, v_n, v_s = north(uu, nu), south(uu, su), north(vv, nv), south(vv, sv)
        r = [pltpu.roll(sv[t], NL - 1, 1) for t in range(NT)]
        sve = [jnp.where(l_last, r[1], r[0]), jnp.where(l_last, c_se, r[1])]
        r = [pltpu.roll(nu[t], 1, 1) for t in range(NT)]
        nuw = [jnp.where(l_first, c_nw, r[0]), jnp.where(l_first, r[0], r[1])]
        a = zipped(jnp.add, vv, v_e)
        v_sum = zipped(jnp.add, a, south(a, [sv[t] + sve[t] for t in range(NT)]))
        b = zipped(jnp.add, uu, u_w)
        u_sum = zipped(jnp.add, b, north(b, [nu[t] + nuw[t] for t in range(NT)]))
        p_e = east(p, p_e)
        p_n = north(p, p_n)

        gu = zipped(lambda w, p, pe, u, ue, uw, vs, un, us: jnp.where(w, (p - pe) - 0.5 * (u * (ue - uw)) - 0.125 * (vs * (un - us)), 0.0),
                    wet_x, p, p_e, uu, u_e, u_w, v_sum, u_n, u_s)
        gv = zipped(lambda w, p, pn, us, ve, vw, v, vn, vs: jnp.where(w, (p - pn) - 0.125 * (us * (ve - vw)) - 0.5 * (v * (vn - vs)), 0.0),
                    wet_y, p, p_n, u_sum, v_e, v_w, vv, v_n, v_s)
        bu = zipped(jnp.add, uu, gu)
        bv = zipped(jnp.add, vv, gv)
        solve(0, m, k, bu, inv_x)
        solve(1, m, k, bv, inv_y)
        for f, (g, b) in enumerate(((gu, bu), (gv, bv))):
            for j in range(NJ):
                for t in range(NT):
                    i = j * NT + t
                    gsum[f, m, i] = gsum[f, m, i] + g[j][t]
                    bsum[f, m, i] = bsum[f, m, i] + b[j][t]
        return cs, cs_n, cs_e

    def momentum_levels(q, carry):
        for h in range(MOM_UNROLL):
            k = q * MOM_UNROLL + h
            mask_x, mask_y = read_mask(1), read_mask(2)
            a1, b1 = tab[0, k], tab[1, k]
            inv = factors(mask_x, k, a1, b1), factors(mask_y, k, a1, b1)
            wet_k = [zipped(lambda n: n > k, mask) for mask in (mask_x, mask_y)]
            carry = tuple(momentum(m, k, carry[m], *wet_k, *inv) for m in range(NM))
        return carry

    start = ([[zero] * NT for _ in range(NJ)], [zero] * NT, [zero] * NJ)
    lax.fori_loop(0, NK // MOM_UNROLL, momentum_levels, (start, start))

    for f in range(2):
        for m in range(NM):
            for t in range(NT):
                for j in range(NJ):
                    fmain.at[m, f, t][pl.ds(j, NS, stride=NJ), :] = gsum[f, m, j * NT + t]
    for m in range(NM):
        pack_side(fside, m, 0, [lambda t, rows, m=m, f=f: fmain[m, f, t, rows] for f in range(2)], lane)
    forces = Exchange(fmain, fside, fwin, fwside, f_send, f_recv, col, row)
    forces.start()

    def tracer(f, m, k, uu, vv, wu, sv, inv_c):
        to_last, to_first = amounts(m, k)
        x = block(f, m, k)
        x_e = east(x, edge(hE, f, to_last))
        x_n = north(x, line(hN, f, m, k))
        w_halo, s_halo = edge(hW, f, to_first), line(hS, f, m, k)
        fx = zipped(lambda u, a, b: u * (a + b), uu, x, x_e)
        fy = zipped(lambda v, a, b: v * (a + b), vv, x, x_n)
        fx_w = west(fx, [wu[j] * (w_halo[j] + x[j][0]) for j in range(NJ)])
        fy_s = south(fy, [sv[t] * (s_halo[t] + x[0][t]) for t in range(NT)])
        solve(f, m, k, zipped(lambda a, f, fw, g, gs: (a + a) - (f - fw) - (g - gs), x, fx, fx_w, fy, fy_s), inv_c)

    def tracer_levels(q, carry):
        for h in range(TRC_UNROLL):
            k = q * TRC_UNROLL + h
            inv_c = factors(read_mask(0), k, tab[2, k], tab[3, k])
            for m in range(NM):
                uu, vv = block(0, m, k), block(1, m, k)
                wu, sv = edge(hW, 0, amounts(m, k)[1]), line(hS, 1, m, k)
                for f in (2, 3):
                    tracer(f, m, k, uu, vv, wu, sv, inv_c)
        return carry

    lax.fori_loop(0, NK // TRC_UNROLL, tracer_levels, 0)

    windows.wait()
    dep = [[window_tile(main, side, 3, j, t, lane, 1, 0) for t in range(WT)] for j in range(WJ)]
    lev = [[window_tile(main, side, 4, j, t, lane, 1, 1) for t in range(WT)] for j in range(WJ)]
    for j in range(WJ):
        row_here = WJ * subl + j
        wall = jnp.logical_and(row_here == 2 * NY - 1, chip == 1)
        dr = [pltpu.roll(dep[j][t], NL - 1, 1) for t in range(WT)]
        lr = [pltpu.roll(lev[j][t], NL - 1, 1) for t in range(WT)]
        for t in range(WT):
            d, k = dep[j][t], lev[j][t]
            de = jnp.where(l_last, dr[(t + 1) % WT], dr[t])
            ke = jnp.where(l_last, lr[(t + 1) % WT], lr[t])
            if j < WJ - 1:
                dn, kn = dep[j + 1][t], lev[j + 1][t]
            else:
                dn, kn = pltpu.roll(dep[0][t], NS - 1, 0), pltpu.roll(lev[0][t], NS - 1, 0)
            kx = jnp.minimum(k, ke)
            ky = jnp.where(wall, 0.0, jnp.minimum(k, kn))
            hx = jnp.where(kx > 0.0, 0.5 * (d + de), 0.0)
            hy = jnp.where(ky > 0.0, 0.5 * (d + dn), 0.0)
            ix = 1.0 / jnp.maximum(kx, 1.0)
            iy = 1.0 / jnp.maximum(ky, 1.0)
            n = j * WT + t
            state[0, n] = window_tile(main, side, 0, j, t, lane, 0, 0)
            for i in (1, 2):
                first = COURANT * window_tile(main, side, i, j, t, lane, 0, i)
                state[i, n] = first
                wi[1 + i, n] = first
            wi[0, n] = (COURANT * COURANT) * hx
            wi[1, n] = (COURANT * COURANT) * hy
            state[3, n] = (COURANT / NSUB) * hx * ix
            state[4, n] = (COURANT / NSUB) * hy * iy
            state[5, n] = zero
            state[6, n] = zero
            if t < NT:
                here = pl.ds(j, NS, stride=WJ)
                nat.at[0, t][here, :] = ix
                nat.at[1, t][here, :] = iy
                nat.at[2, t][here, :] = 1.0 / jnp.where(kx > 0.0, hx, 1.0)
                nat.at[3, t][here, :] = 1.0 / jnp.where(ky > 0.0, hy, 1.0)
    own = pl.ds(pl.multiple_of(core * NY, NS), NY)
    for t in range(NT):
        for i in range(4):
            rl[i, t] = nat[i, t, own]

    def tail(i, carry):
        s1, s2, n = carry
        w = weights[NSUB - 1 - i]
        return s1 + w, s2 + n * w, n - 1.0

    total, moment, _ = lax.fori_loop(0, NSUB, tail, (0.0, 0.0, float(NSUB)))
    edge_wall = jnp.where(jnp.logical_and(s_first, chip == 0), 0.0, 1.0)
    forces.wait()
    for j in range(WJ):
        for t in range(WT):
            n = j * WT + t
            for f in range(2):
                state[3 + f, n] = state[3 + f, n] * window_tile(fwin, fwside, f, j, t, lane, 0, f)

    def subcycle(i, remain):
        w = weights[i]
        for j in range(WJ):
            r = [pltpu.roll(state[1, j * WT + t], 1, 1) for t in range(WT)]
            for t in range(WT):
                n = j * WT + t
                uw = jnp.where(l_first, r[(t + WT - 1) % WT], r[t])
                if j == 0:
                    vs = pltpu.roll(state[2, (WJ - 1) * WT + t], 1, 0) * edge_wall
                else:
                    vs = state[2, n - WT]
                e = state[0, n] - ((state[1, n] - uw) + (state[2, n] - vs))
                state[0, n] = e
                state[5, n] = state[5, n] + w * e
                state[6, n] = state[6, n] + remain * e
        for j in range(WJ):
            e = [state[0, j * WT + t] for t in range(WT)]
            r = [pltpu.roll(e[t], NL - 1, 1) for t in range(WT)]
            for t in range(WT):
                n = j * WT + t
                ee = jnp.where(l_last, r[(t + 1) % WT], r[t])
                if j == WJ - 1:
                    en = pltpu.roll(state[0, t], NS - 1, 0)
                else:
                    en = state[0, n + WT]
                state[1, n] = (state[1, n] + state[3, n]) - wi[0, n] * (ee - e[t])
                state[2, n] = (state[2, n] + state[4, n]) - wi[1, n] * (en - e[t])
        return remain - w

    lax.fori_loop(0, NSUB, subcycle, total)

    scale = 1.0 / COURANT
    for j in range(WJ):
        q = [state[6, j * WT + t] for t in range(WT)]
        r = [pltpu.roll(q[t], NL - 1, 1) for t in range(WT)]
        for t in range(NT):
            n = j * WT + t
            qe = jnp.where(l_last, r[t + 1], r[t])
            qn = pltpu.roll(state[6, t], NS - 1, 0) if j == WJ - 1 else state[6, n + WT]
            here = pl.ds(j, NS, stride=WJ)
            res.at[0, t][here, :] = state[5, n]
            res.at[1, t][here, :] = scale * (total * wi[2, n] + moment * state[3, n] - wi[0, n] * (qe - q[t]))
            res.at[2, t][here, :] = scale * (total * wi[3, n] + moment * state[4, n] - wi[1, n] * (qn - q[t]))
    other = 1 - core
    send = remote(res.at[:, :, pl.ds(pl.multiple_of(other * NY, NS), NY)], out.at[core], out_send, out_recv, col, chip * 2 + other)
    send.start()
    keep = pltpu.make_async_copy(res.at[:, :, pl.ds(pl.multiple_of(core * NY, NS), NY)], out.at[core], loc_sem)
    keep.start()
    keep.wait()
    send.wait()


def step_call(vel_x, vel_y, pot_temp, salinity, surf_eta, trans_x, trans_y, col_depth, wet_levels, weights, tab):
    dma = pltpu.SemaphoreType.DMA
    nreg = NJ * NT
    nwin = WJ * WT

    def vm(*shape):
        return pltpu.VMEM(shape, F32)

    return pl.pallas_call(
        step_kernel,
        out_shape=(
            vm(4, NM, NK + 1, nreg, *VR),
            vm(2, NM, nreg, *VR),
            pltpu.VMEM((3, nreg, *VR), jnp.int32),
            vm(4, NT, NY, NL),
            vm(NM, 3, NT, NY, NL),
        ),
        in_specs=[ANY] * 4 + [VM] * 5 + [SM] * 2,
        out_specs=(VM,) * 5,
        scratch_shapes=[
            vm(4, NM, NT, NK, NY, NL),
            vm(4, NY, NL), vm(4, NY, NL), vm(4, NT, NM * NK, NL), vm(4, NT, NM * NK, NL), vm(*VR), vm(*VR),
            vm(4, NY, NL), vm(4, NY, NL), vm(4, NT, NM * NK, NL), vm(4, NT, NM * NK, NL),
            vm(NT, NY, NL), vm(NY, NL), vm(NT, *VR),
            vm(NM, 5, NT, NY, NL), vm(NM, 2, 2, NY, NL), vm(5, NT, WY, NL), vm(2, 2, WY, NL),
            vm(2, NM, nreg, *VR),
            vm(NM, 2, NT, NY, NL), vm(NM, 2, 1, NY, NL), vm(2, NT, WY, NL), vm(2, 1, WY, NL),
            vm(4, nwin, *VR), vm(4, NT, WY, NL), vm(7, nwin, *VR), vm(3, NT, WY, NL),
            dma((4, NM, NT, NC)), dma((2, 4)), dma((4,)), dma((4,)), dma((2, 4)), dma((4,)), dma((4,)), dma((2,)), dma((2,)), dma((2,)), dma((2,)),
            dma((16,)), dma((2,)), dma((16,)), dma((2,)), dma, dma, dma,
        ],
        compiler_params=pltpu.CompilerParams(collective_id=0, has_side_effects=True, vmem_limit_bytes=VMEM_LIMIT),
        name="ocean_step",
    )(vel_x, vel_y, pot_temp, salinity, surf_eta, trans_x, trans_y, col_depth, wet_levels, weights, tab)


def final_kernel(sbuf, bsum, kl, rl, bo, tab, eta_out, tx_out, ty_out, u_out, v_out, temp_out, salt_out, xbuf, cor, out_sem):
    outs = (u_out, v_out, temp_out, salt_out)

    def store(f, m, t, c):
        part = pl.ds(c * CH, CH)
        return pltpu.make_async_copy(xbuf.at[f, m, t, part], outs[f].at[part, m, :, pl.ds(t * NL, NL)], out_sem.at[f, m, t, c])

    def each_store(fs, c, op):
        for f in fs:
            for m in range(NM):
                for t in range(NT):
                    getattr(store(f, m, t, c), op)()

    zero = jnp.zeros(VR, F32)
    for m in range(NM):
        for t in range(NT):
            cols = pl.ds(t * NL, NL)
            eta_out[m, :, cols] = bo[m, 0, t]
            tx_out[m, :, cols] = bo[m, 1, t]
            ty_out[m, :, cols] = bo[m, 2, t]
            for f in range(2):
                for j in range(NJ):
                    here = pl.ds(j, NS, stride=NJ)
                    i = j * NT + t
                    cor[f, m, i] = bo.at[m, 1 + f, t][here, :] * rl.at[2 + f, t][here, :] - bsum[f, m, i] * rl.at[f, t][here, :]

    def back(fs):
        def chunk(c2, xs):
            c = NC - 1 - c2

            def step(q, xs):
                xs = list(xs)
                for h in range(2):
                    k = c * CH + CH - 1 - 2 * q - h
                    n = 0
                    for f in fs:
                        g = tab[f // 2 * 2, k]
                        for j in range(NJ):
                            for t in range(NT):
                                here = pl.ds(j, NS, stride=NJ)
                                i = j * NT + t
                                if f < 2:
                                    wet = kl[1 + f, i] > k
                                for m in range(NM):
                                    x = sbuf[f, m, k + 1, i] + g * xs[n]
                                    xs[n] = x
                                    n += 1
                                    xbuf.at[f, m, t, k][here, :] = jnp.where(wet, x + cor[f, m, i], 0.0) if f < 2 else x
                return tuple(xs)

            xs = lax.fori_loop(0, CH // 2, step, xs)
            each_store(fs, c, "start")
            return xs

        lax.fori_loop(0, NC, chunk, (zero,) * (len(fs) * NM * NJ * NT))

    back((2, 3))
    back((0, 1))

    def drain(c, _):
        each_store(range(4), c, "wait")
        return 0

    lax.fori_loop(0, NC, drain, 0)


def final_call(sbuf, bsum, kl, rl, bo, tab):
    flat = jax.ShapeDtypeStruct((NM, NY, NX), F32)
    block = jax.ShapeDtypeStruct((NK, NM, NY, NX), F32)
    held = [pltpu.with_memory_space_constraint(x, pltpu.VMEM) for x in (sbuf, bsum, kl, rl, bo)]
    return pl.pallas_call(
        final_kernel,
        out_shape=(flat,) * 3 + (block,) * 4,
        in_specs=[VM] * 5 + [SM],
        out_specs=(VM,) * 3 + (ANY,) * 4,
        scratch_shapes=[
            pltpu.VMEM((4, NM, NT, NK, NY, NL), F32),
            pltpu.VMEM((2, NM, NJ * NT, *VR), F32),
            pltpu.SemaphoreType.DMA((4, NM, NT, NC)),
        ],
        compiler_params=pltpu.CompilerParams(vmem_limit_bytes=VMEM_LIMIT),
        name="back_substitution",
    )(*held, tab)


def solution(mesh):
    def local_step(*args):
        tab = level_table()
        sbuf, bsum, kl, rl, bo = step_call(*args, tab)
        return final_call(sbuf, bsum, kl, rl, bo, tab)

    spec_3d = P(None, None, "row", "col")
    spec_2d = P(None, "row", "col")
    spec_map = P("row", "col")
    return jax.shard_map(local_step, mesh=mesh, in_specs=(spec_3d,) * 4 + (spec_2d,) * 3 + (spec_map,) * 2 + (P(),), out_specs=(spec_2d,) * 3 + (spec_3d,) * 4, check_vma=False)
```

profile of v0, /device:TPU:0, one launch (start us, length us, event | category | flops | bytes accessed | tf_op | source)
XLA Modules:
  0.0 69.0 jit_solution(2273394323915690716)
XLA Ops:
  0.6 60.4 %ocean_step.1 = (f32[4,2,61,8,8,128]{5,4,3,2,1,0:T(8,128)S(1)}, f32[2,2,8,8,128]{4,3,2,1,0:T(8,128)S(1)}, s32[3,8,8,128]{3,2,1,0:T(8,128)S(1)}, f32[4,2,32,128]{3,2,1,0:T(8,128)S(1)}, f32[2,3,2,32,128]{4,3,2,1,0:T(8,128)S(1)}) custom-call(f32[60,2,32,256]{3,2,1,0:T(8,128)} %u.1, f32[60,2,32,256]{3,2,1,0:T(8,128)} %v.1, f32[60,2,32,256]{3,2,1,0:T(8,128)} %temp.1, ...), custom_call_target="tpu_custom_call" | custom-call | tf_op jit(solution)/shard_map/ocean_step/pallas_call | solution.py:606
  61.0 8.0 %back_substitution.1 = (f32[2,32,256]{2,1,0:T(8,128)}, f32[2,32,256]{2,1,0:T(8,128)}, f32[2,32,256]{2,1,0:T(8,128)}, f32[60,2,32,256]{3,2,1,0:T(8,128)}, f32[60,...) custom-call(f32[4,2,61,8,8,128]{5,4,3,2,1,0:T(8,128)S(1)} %get-tuple-element.12.sbuf, ...), custom_call_target="tpu_custom_call" | custom-call | tf_op jit(solution)/shard_map/back_substitution/pallas_call | solution.py:704
where the time goes:
time: 69.2 us; the launch traced here: 69 us
  Pallas kernels  68.4 us (99%)
    pallas_call x1, Pallas kernels, step_call(): pl.pallas_call(step_kernel, out_shape=(vm(4, NM, NK + 1, nreg, *VR), vm(2...  60.4 us
    pallas_call x1, Pallas kernels, final_call(): pl.pallas_call(final_kernel, out_shape=(flat,) * 3 + (block,) * 4, in_spe...  8.04 us

commit v1 on v0

--- a/solution.py
+++ b/solution.py
@@ -155,13 +155,13 @@
 
 PA = 0.15 * 0.5 / NK * 0.5
 PB = 0.2 * 0.5 / NK * 0.5
-MOM_UNROLL = 1
-TRC_UNROLL = 3
+MOM_UNROLL = 2
+TRC_UNROLL = 2
 
 
 def step_kernel(u, v, temp, salt, eta, tx, ty, depth, wet, weights, tab,
                 sbuf, bsum, kl, rl, out,
-                inb, hE, hW, hN, hS, hSE, hNW, colF, colL, rowF, rowL, ksrc, kE, kN,
+                inb, ew, ends, corner, sv_east, nu_west, uw_all, hE, hW, hN, hS, hSE, hNW, colF, colL, rowF, rowL, ksrc, kE, kN,
                 wmain, wside, main, side, gsum, fmain, fside, fwin, fwside, wi, nat, state, res,
                 in_sem, sendC, recvE, recvW, sendR, recvN, recvS, corn_send, corn_recv, k_send, k_recv,
                 w_send, w_recv, f_send, f_recv, out_send, out_recv, loc_sem):
@@ -225,7 +225,6 @@
     def _():
         k_south.start()
 
-    half_lane = NL // 2
     for f in range(4):
         def chunk(c, acc, f=f):
             each_load(f, c, "wait")
@@ -233,7 +232,7 @@
             for q in range(CH):
                 k = c * CH + q
                 for m in range(NM):
-                    spot = k + half_lane * m
+                    spot = 2 * k + m
                     hit = lane == spot
                     for i in range(NJ):
                         rows = pl.ds(i * NS, NS)
@@ -331,6 +330,22 @@
             to_north(f).wait_send()
             to_south(f).wait_recv()
 
+    odd = lax.rem(lane, 2)
+    for m in range(NM):
+        for f in range(4):
+            for i in range(NJ):
+                rows = pl.ds(i * NS, NS)
+                ew[f, m, rows] = jnp.where(odd == m, hE[f, rows], pltpu.roll(hW[f, rows], 1, 1))
+        corner[m] = jnp.where(odd == m, hSE[pl.ds(NS - 1, NS, stride=0), :], pltpu.roll(hNW[pl.ds(0, NS, stride=0), :], 1, 1))
+    for i in range(NM * NK // NS):
+        rows = pl.ds(i * NS, NS)
+        r = [pltpu.roll(hS[1, t, rows], NL - 1, 1) for t in range(NT)]
+        sv_east[0, rows] = jnp.where(l_last, r[1], r[0])
+        sv_east[1, rows] = r[1]
+        r = [pltpu.roll(hN[0, t, rows], 1, 1) for t in range(NT)]
+        nu_west[0, rows] = r[0]
+        nu_west[1, rows] = jnp.where(l_first, r[0], r[1])
+
     def rolls(x, amount):
         return [[pltpu.roll(x[j][t], amount, 1) for t in range(NT)] for j in range(NJ)]
 
@@ -371,14 +386,8 @@
     def block(f, m, k):
         return [[inb.at[f, m, t, k][pl.ds(j, NS, stride=NJ), :] for t in range(NT)] for j in range(NJ)]
 
-    def line(ref, f, m, k):
-        return [ref.at[f, t][pl.ds(m * NK + k, NS, stride=0), :] for t in range(NT)]
-
-    def amounts(m, k):
-        return NL - 1 - half_lane * m - k, lax.rem(NL - half_lane * m - k, NL)
-
-    def edge(ref, f, amount):
-        return [pltpu.roll(x, amount, 1) for x in strided(ref.at[f])]
+    def line(ref, m, k):
+        return [ref.at[t][pl.ds(m * NK + k, NS, stride=0), :] for t in range(NT)]
 
     def solve(f, m, k, side_k, scale):
         for j in range(NJ):
@@ -389,13 +398,14 @@
     def momentum(m, k, carry, wet_x, wet_y, inv_x, inv_y):
         cs, cs_n, cs_e = carry
         uu, vv, tt, ss = (block(f, m, k) for f in range(4))
-        to_last, to_first = amounts(m, k)
-        eu, ev, et, es = (edge(hE, f, to_last) for f in range(4))
-        wu, wv = (edge(hW, f, to_first) for f in range(2))
-        nu, nv, nt, ns = (line(hN, f, m, k) for f in range(4))
-        su, sv = (line(hS, f, m, k) for f in range(2))
-        c_se = pltpu.roll(hSE[pl.ds(NS - 1, NS, stride=0), :], to_last, 1)
-        c_nw = pltpu.roll(hNW[pl.ds(0, NS, stride=0), :], to_first, 1)
+        amount = NL - 1 - m - 2 * k
+        eu, ev, et, es = ([pltpu.roll(x, amount, 1) for x in strided(ew.at[f, m])] for f in range(4))
+        c = pltpu.roll(corner[m], amount, 1)
+        for j in range(NJ):
+            ends[0, m, k, j] = et[j]
+            ends[1, m, k, j] = es[j]
+        nu, nv, nt, ns = (line(hN.at[f], m, k) for f in range(4))
+        su, sv = (line(hS.at[f], m, k) for f in range(2))
 
         half = zipped(lambda s, t: PA * s - PB * t, ss, tt)
         p = zipped(jnp.add, cs, half)
@@ -407,12 +417,14 @@
         p_e = [cs_e[j] + half_e[j] for j in range(NJ)]
         cs_e = [p_e[j] + half_e[j] for j in range(NJ)]
 
-        u_e, u_w, v_e, v_w = east(uu, eu), west(uu, wu), east(vv, ev), west(vv, wv)
+        u_e, u_w, v_e, v_w = east(uu, eu), west(uu, eu), east(vv, ev), west(vv, ev)
+        for j in range(NJ):
+            for t in range(NT):
+                uw_all[m, k, j * NT + t] = u_w[j][t]
         u_n, u_s, v_n, v_s = north(uu, nu), south(uu, su), north(vv, nv), south(vv, sv)
-        r = [pltpu.roll(sv[t], NL - 1, 1) for t in range(NT)]
-        sve = [jnp.where(l_last, r[1], r[0]), jnp.where(l_last, c_se, r[1])]
-        r = [pltpu.roll(nu[t], 1, 1) for t in range(NT)]
-        nuw = [jnp.where(l_first, c_nw, r[0]), jnp.where(l_first, r[0], r[1])]
+        sve, nuw = line(sv_east, m, k), line(nu_west, m, k)
+        sve[1] = jnp.where(l_last, c, sve[1])
+        nuw[0] = jnp.where(l_first, c, nuw[0])
         a = zipped(jnp.add, vv, v_e)
         v_sum = zipped(jnp.add, a, south(a, [sv[t] + sve[t] for t in range(NT)]))
         b = zipped(jnp.add, uu, u_w)
@@ -459,15 +471,15 @@
     forces = Exchange(fmain, fside, fwin, fwside, f_send, f_recv, col, row)
     forces.start()
 
-    def tracer(f, m, k, uu, vv, wu, sv, inv_c):
-        to_last, to_first = amounts(m, k)
+    def tracer(f, m, k, uu, vv, u_w, sv, inv_c):
         x = block(f, m, k)
-        x_e = east(x, edge(hE, f, to_last))
-        x_n = north(x, line(hN, f, m, k))
-        w_halo, s_halo = edge(hW, f, to_first), line(hS, f, m, k)
+        halo = [ends[f - 2, m, k, j] for j in range(NJ)]
+        x_e, x_w = east(x, halo), west(x, halo)
+        x_n = north(x, line(hN.at[f], m, k))
+        s_halo = line(hS.at[f], m, k)
         fx = zipped(lambda u, a, b: u * (a + b), uu, x, x_e)
+        fx_w = zipped(lambda u, a, b: u * (a + b), u_w, x, x_w)
         fy = zipped(lambda v, a, b: v * (a + b), vv, x, x_n)
-        fx_w = west(fx, [wu[j] * (w_halo[j] + x[j][0]) for j in range(NJ)])
         fy_s = south(fy, [sv[t] * (s_halo[t] + x[0][t]) for t in range(NT)])
         solve(f, m, k, zipped(lambda a, f, fw, g, gs: (a + a) - (f - fw) - (g - gs), x, fx, fx_w, fy, fy_s), inv_c)
 
@@ -476,10 +488,10 @@
             k = q * TRC_UNROLL + h
             inv_c = factors(read_mask(0), k, tab[2, k], tab[3, k])
             for m in range(NM):
-                uu, vv = block(0, m, k), block(1, m, k)
-                wu, sv = edge(hW, 0, amounts(m, k)[1]), line(hS, 1, m, k)
+                uu, vv, sv = block(0, m, k), block(1, m, k), line(hS.at[1], m, k)
+                u_w = [[uw_all[m, k, j * NT + t] for t in range(NT)] for j in range(NJ)]
                 for f in (2, 3):
-                    tracer(f, m, k, uu, vv, wu, sv, inv_c)
+                    tracer(f, m, k, uu, vv, u_w, sv, inv_c)
         return carry
 
     lax.fori_loop(0, NK // TRC_UNROLL, tracer_levels, 0)
@@ -616,6 +628,7 @@
         out_specs=(VM,) * 5,
         scratch_shapes=[
             vm(4, NM, NT, NK, NY, NL),
+            vm(4, NM, NY, NL), vm(2, NM, NK, NJ, *VR), vm(NM, *VR), vm(NT, NM * NK, NL), vm(NT, NM * NK, NL), vm(NM, NK, nreg, *VR),
             vm(4, NY, NL), vm(4, NY, NL), vm(4, NT, NM * NK, NL), vm(4, NT, NM * NK, NL), vm(*VR), vm(*VR),
             vm(4, NY, NL), vm(4, NY, NL), vm(4, NT, NM * NK, NL), vm(4, NT, NM * NK, NL),
             vm(NT, NY, NL), vm(NY, NL), vm(NT, *VR),

time: 69.2 us -> 56.5 us (0.82)
  Pallas kernels: 68.4 us -> 55.7 us
    pallas_call x1, Pallas kernels: 60.4 us -> 47.7 us  [step_call(): pl.pallas_call(step_kernel, out_shape=(vm(4, NM, NK + 1, nreg, *VR), vm(2...]
where the time goes in v1:
time: 56.5 us; the launch traced here: 56.3 us
  Pallas kernels  55.7 us (99%)
  between operations  0.64 us (1%)
    pallas_call x1, Pallas kernels, step_call(): pl.pallas_call(step_kernel, out_shape=(vm(4, NM, NK + 1, nreg, *VR), vm(2...  47.7 us
    pallas_call x1, Pallas kernels, final_call(): pl.pallas_call(final_kernel, out_shape=(flat,) * 3 + (block,) * 4, in_spe...  8.04 us

profile of v1, /device:TPU:0, one launch (start us, length us, event | category | flops | bytes accessed | tf_op | source)
XLA Modules:
  0.0 56.3 jit_solution(16095650556834950883)
XLA Ops:
  0.6 47.7 %ocean_step.1 = (f32[4,2,61,8,8,128]{5,4,3,2,1,0:T(8,128)S(1)}, f32[2,2,8,8,128]{4,3,2,1,0:T(8,128)S(1)}, s32[3,8,8,128]{3,2,1,0:T(8,128)S(1)}, f32[4,2,32,128]{3,2,1,0:T(8,128)S(1)}, f32[2,3,2,32,128]{4,3,2,1,0:T(8,128)S(1)}) custom-call(f32[60,2,32,256]{3,2,1,0:T(8,128)} %u.1, f32[60,2,32,256]{3,2,1,0:T(8,128)} %v.1, f32[60,2,32,256]{3,2,1,0:T(8,128)} %temp.1, ...), custom_call_target="tpu_custom_call" | custom-call | tf_op jit(solution)/shard_map/ocean_step/pallas_call | solution.py:618
  48.3 8.0 %back_substitution.1 = (f32[2,32,256]{2,1,0:T(8,128)}, f32[2,32,256]{2,1,0:T(8,128)}, f32[2,32,256]{2,1,0:T(8,128)}, f32[60,2,32,256]{3,2,1,0:T(8,128)}, f32[60,...) custom-call(f32[4,2,61,8,8,128]{5,4,3,2,1,0:T(8,128)S(1)} %get-tuple-element.12.sbuf, ...), custom_call_target="tpu_custom_call" | custom-call | tf_op jit(solution)/shard_map/back_substitution/pallas_call | solution.py:717

commit v2 on v1

--- a/solution.py
+++ b/solution.py
@@ -15,6 +15,7 @@
 NL = 128
 NS = 8
 VR = (NS, NL)
+NF = 4
 NX = 256
 NT = NX // NL
 NJ = NY // 8
@@ -26,12 +27,13 @@
 WT = 3
 NSUB = 40
 COURANT = 0.4
-VMEM_LIMIT = 42 << 20
+VMEM_LIMIT = 28 << 20
+STEP_LIMIT = 28 << 20
 SIDE = 40
 
 VM = pl.BlockSpec(memory_space=pltpu.VMEM)
 SM = pl.BlockSpec(memory_space=pltpu.SMEM)
-ANY = pl.BlockSpec(memory_space=pl.ANY)
+HBM = pl.BlockSpec(memory_space=pl.ANY)
 
 
 def level_table():
@@ -66,12 +68,12 @@
     barrier = pltpu.get_barrier_semaphore()
     count = 0
     for dc in (0, 1, 3):
-        for dr in range(4):
+        for dr in range(NF):
             if dc == 0 and dr == 0:
                 continue
             pl.semaphore_signal(barrier, inc=1, device_id=device(lax.rem(col + dc, 4), lax.rem(row + dr, 4)), device_id_type=MESH)
             count += 1
-    pl.semaphore_wait(barrier, count)
+    return lambda: pl.semaphore_wait(barrier, count)
 
 
 class Exchange:
@@ -156,12 +158,94 @@
 PA = 0.15 * 0.5 / NK * 0.5
 PB = 0.2 * 0.5 / NK * 0.5
 MOM_UNROLL = 2
-TRC_UNROLL = 2
+TRC_UNROLL = 4
+SUB_UNROLL = 1
+
+
+def rolls(x, amount):
+    return [[pltpu.roll(x[j][t], amount, 1) for t in range(NT)] for j in range(NJ)]
+
+
+def east(x, halo):
+    edge, r = lanes_iota() == NL - 1, rolls(x, NL - 1)
+    return [[jnp.where(edge, r[j][1] if t == 0 else halo[j], r[j][t]) for t in range(NT)] for j in range(NJ)]
+
+
+def west(x, halo):
+    edge, r = lanes_iota() == 0, rolls(x, 1)
+    return [[jnp.where(edge, r[j][0] if t == 1 else halo[j], r[j][t]) for t in range(NT)] for j in range(NJ)]
+
+
+def north(x, halo):
+    edge = subl_iota() == NS - 1
+    return x[1:] + [[jnp.where(edge, halo[t], pltpu.roll(x[0][t], NS - 1, 0)) for t in range(NT)]]
+
+
+def south(x, halo):
+    edge = subl_iota() == 0
+    return [[jnp.where(edge, halo[t], pltpu.roll(x[NJ - 1][t], 1, 0)) for t in range(NT)]] + x[:-1]
+
+
+def zipped(fn, *xs):
+    return [[fn(*[x[j][t] for x in xs]) for t in range(NT)] for j in range(NJ)]
+
+
+def strided(ref):
+    return [ref[pl.ds(j, NS, stride=NJ), :] for j in range(NJ)]
+
+
+def read_mask(kl, n):
+    return [[kl[n, j * NT + t] for t in range(NT)] for j in range(NJ)]
+
+
+def factors(mask, k, a, b):
+    return zipped(lambda n: jnp.where(n > k + 1, a, jnp.where(n == k + 1, b, 0.0)), mask)
+
+
+def read_block(ref, index, k):
+    return [[ref.at[(*index, t, k)][pl.ds(j, NS, stride=NJ), :] for t in range(NT)] for j in range(NJ)]
+
+
+def line(ref, m, k):
+    return [ref.at[t][pl.ds(m * NK + k, NS, stride=0), :] for t in range(NT)]
+
+
+def solve(sbuf, f, m, k, side, scale):
+    for j in range(NJ):
+        for t in range(NT):
+            i = j * NT + t
+            sbuf[f, m, k + 1, i] = (side[j][t] + sbuf[f, m, k, i]) * scale[j][t]
+
+
+def tracer_pass(inb, field, ends, uw_all, north_rows, south_rows, south_v, kl, tab, sbuf, f):
+    def level(m, k, inv_c):
+        uu, vv, sv = read_block(inb, (0, m), k), read_block(inb, (1, m), k), line(south_v, m, k)
+        u_w = [[uw_all[m, k, j * NT + t] for t in range(NT)] for j in range(NJ)]
+        x = read_block(*field(m), k)
+        halo = [ends[m, k, j] for j in range(NJ)]
+        x_e, x_w = east(x, halo), west(x, halo)
+        x_n = north(x, line(north_rows, m, k))
+        x_s = line(south_rows, m, k)
+        fx = zipped(lambda u, a, b: u * (a + b), uu, x, x_e)
+        fx_w = zipped(lambda u, a, b: u * (a + b), u_w, x, x_w)
+        fy = zipped(lambda v, a, b: v * (a + b), vv, x, x_n)
+        fy_s = south(fy, [sv[t] * (x_s[t] + x[0][t]) for t in range(NT)])
+        solve(sbuf, f, m, k, zipped(lambda a, b, bw, g, gs: (a + a) - (b - bw) - (g - gs), x, fx, fx_w, fy, fy_s), inv_c)
+
+    def levels(q, carry):
+        for h in range(TRC_UNROLL):
+            k = q * TRC_UNROLL + h
+            inv_c = factors(read_mask(kl, 0), k, tab[2, k], tab[3, k])
+            for m in range(NM):
+                level(m, k, inv_c)
+        return carry
+
+    lax.fori_loop(0, NK // TRC_UNROLL, levels, 0)
 
 
 def step_kernel(u, v, temp, salt, eta, tx, ty, depth, wet, weights, tab,
-                sbuf, bsum, kl, rl, out,
-                inb, ew, ends, corner, sv_east, nu_west, uw_all, hE, hW, hN, hS, hSE, hNW, colF, colL, rowF, rowL, ksrc, kE, kN,
+                sbuf, bsum, kl, rl, out, inb, ends_s, uw_all, hN, hS,
+                inb_t, ew, ends_t, corner, sv_east, nu_west, hE, hW, hSE, hNW, colF, colL, rowF, rowL, ksrc, kE, kN,
                 wmain, wside, main, side, gsum, fmain, fside, fwin, fwside, wi, nat, state, res,
                 in_sem, sendC, recvE, recvW, sendR, recvN, recvS, corn_send, corn_recv, k_send, k_recv,
                 w_send, w_recv, f_send, f_recv, out_send, out_recv, loc_sem):
@@ -182,23 +266,29 @@
     s_last, s_first = subl == NS - 1, subl == 0
     zero = jnp.zeros(VR, F32)
 
+    def place(f, *index):
+        return inb_t.at[index] if f == 2 else inb.at[(min(f, 2), *index)]
+
+    def held(f, *index):
+        return inb_t[index] if f == 2 else inb[(min(f, 2), *index)]
+
     def load(f, m, t, c):
         part = pl.ds(c * CH, CH)
-        return pltpu.make_async_copy(fields[f].at[part, m, :, pl.ds(t * NL, NL)], inb.at[f, m, t, part], in_sem.at[f, m, t, c])
+        return pltpu.make_async_copy(fields[f].at[part, m, :, pl.ds(t * NL, NL)], place(f, m, t, part), in_sem.at[f, m, t, c])
 
     def each_load(f, c, op):
         for m in range(NM):
             for t in range(NT):
                 getattr(load(f, m, t, c), op)()
 
-    for f in range(4):
+    for f in range(NF):
         for c in range(NC):
             each_load(f, c, "start")
 
     for t in range(NT):
         ksrc[t] = wet[:, pl.ds(t * NL, NL)].astype(F32)
 
-    greet(col, row)
+    greet(col, row)()
 
     def remote(s, d, ssem, rsem, dc, dr):
         return pltpu.make_async_remote_copy(src_ref=s, dst_ref=d, send_sem=ssem, recv_sem=rsem, device_id=device(dc, dr), device_id_type=MESH)
@@ -219,13 +309,8 @@
     corner_north = remote(colF.at[1, pl.ds(NY - NS, NS)], hSE, corn_send.at[0], corn_recv.at[0], west_dev, north_dev)
     corner_south = remote(colL.at[0, pl.ds(0, NS)], hNW, corn_send.at[1], corn_recv.at[1], east_dev, south_dev)
 
-    k_west.start()
-
-    @pl.when(has_south)
-    def _():
-        k_south.start()
-
-    for f in range(4):
+    lane_next = lax.rem(lane + 1, NL)
+    for f in range(NF):
         def chunk(c, acc, f=f):
             each_load(f, c, "wait")
             acc = list(acc)
@@ -233,22 +318,27 @@
                 k = c * CH + q
                 for m in range(NM):
                     spot = 2 * k + m
-                    hit = lane == spot
+                    hit, hit_last = lane == spot, lane_next == spot
                     for i in range(NJ):
                         rows = pl.ds(i * NS, NS)
-                        first = pltpu.roll(inb[f, m, 0, k, rows], spot, 1)
-                        last = pltpu.roll(inb[f, m, NT - 1, k, rows], lax.rem(spot + 1, NL), 1)
-                        acc[2 * i] = jnp.where(hit, first, acc[2 * i])
-                        acc[2 * i + 1] = jnp.where(hit, last, acc[2 * i + 1])
+                        both = pltpu.roll(jnp.where(l_first, held(f, m, 0, k, rows), held(f, m, NT - 1, k, rows)), spot, 1)
+                        acc[2 * i] = jnp.where(hit, both, acc[2 * i])
+                        acc[2 * i + 1] = jnp.where(hit_last, both, acc[2 * i + 1])
                     for t in range(NT):
-                        rowF[f, t, pl.ds(m * NK + k, 1), :] = inb[f, m, t, k, 0:1]
-                        rowL[f, t, pl.ds(m * NK + k, 1), :] = inb[f, m, t, k, NY - 1:NY]
+                        rowF[f, t, pl.ds(m * NK + k, 1), :] = held(f, m, t, k, pl.ds(0, 1))
+                        rowL[f, t, pl.ds(m * NK + k, 1), :] = held(f, m, t, k, pl.ds(NY - 1, 1))
             return tuple(acc)
 
         acc = lax.fori_loop(0, NC, chunk, (zero,) * (2 * NJ))
         for i in range(NJ):
             colF[f, pl.ds(i * NS, NS)] = acc[2 * i]
             colL[f, pl.ds(i * NS, NS)] = acc[2 * i + 1]
+        if f == 0:
+            k_west.start()
+
+            @pl.when(has_south)
+            def _():
+                k_south.start()
 
         @pl.when(has_south)
         def _():
@@ -292,7 +382,7 @@
         hS[...] = jnp.zeros(hS.shape, F32)
         hSE[...] = jnp.zeros(hSE.shape, F32)
 
-    for f in range(4):
+    for f in range(3):
         for m in range(NM):
             for i in range(NJ * NT):
                 sbuf[f, m, 0, i] = zero
@@ -316,7 +406,7 @@
         corner_north.wait_send()
         corner_south.wait_recv()
 
-    for f in range(4):
+    for f in range(NF):
         for copy in col_copies(f):
             copy.wait()
 
@@ -332,11 +422,11 @@
 
     odd = lax.rem(lane, 2)
     for m in range(NM):
-        for f in range(4):
+        for f in range(NF):
             for i in range(NJ):
                 rows = pl.ds(i * NS, NS)
-                ew[f, m, rows] = jnp.where(odd == m, hE[f, rows], pltpu.roll(hW[f, rows], 1, 1))
-        corner[m] = jnp.where(odd == m, hSE[pl.ds(NS - 1, NS, stride=0), :], pltpu.roll(hNW[pl.ds(0, NS, stride=0), :], 1, 1))
+                ew[f, m, rows] = jnp.where(odd == m, hE[f, rows], pltpu.roll(hW[f, rows], 2, 1))
+        corner[m] = jnp.where(odd == m, hSE[pl.ds(NS - 1, NS, stride=0), :], pltpu.roll(hNW[pl.ds(0, NS, stride=0), :], 2, 1))
     for i in range(NM * NK // NS):
         rows = pl.ds(i * NS, NS)
         r = [pltpu.roll(hS[1, t, rows], NL - 1, 1) for t in range(NT)]
@@ -346,29 +436,6 @@
         nu_west[0, rows] = r[0]
         nu_west[1, rows] = jnp.where(l_first, r[0], r[1])
 
-    def rolls(x, amount):
-        return [[pltpu.roll(x[j][t], amount, 1) for t in range(NT)] for j in range(NJ)]
-
-    def east(x, halo):
-        r = rolls(x, NL - 1)
-        return [[jnp.where(l_last, r[j][1] if t == 0 else halo[j], r[j][t]) for t in range(NT)] for j in range(NJ)]
-
-    def west(x, halo):
-        r = rolls(x, 1)
-        return [[jnp.where(l_first, r[j][0] if t == 1 else halo[j], r[j][t]) for t in range(NT)] for j in range(NJ)]
-
-    def north(x, halo):
-        return x[1:] + [[jnp.where(s_last, halo[t], pltpu.roll(x[0][t], NS - 1, 0)) for t in range(NT)]]
-
-    def south(x, halo):
-        return [[jnp.where(s_first, halo[t], pltpu.roll(x[NJ - 1][t], 1, 0)) for t in range(NT)]] + x[:-1]
-
-    def zipped(fn, *xs):
-        return [[fn(*[x[j][t] for x in xs]) for t in range(NT)] for j in range(NJ)]
-
-    def strided(ref):
-        return [ref[pl.ds(j, NS, stride=NJ), :] for j in range(NJ)]
-
     k_mid = zipped(lambda x: x, [list(pair) for pair in zip(*[strided(ksrc.at[t]) for t in range(NT)])])
     k_east = zipped(jnp.minimum, k_mid, east(k_mid, [pltpu.roll(x, NL - 1, 1) for x in strided(kE)]))
     k_north = zipped(jnp.minimum, k_mid, north(k_mid, [kN.at[t][pl.ds(0, NS, stride=0), :] for t in range(NT)]))
@@ -377,34 +444,19 @@
             for t in range(NT):
                 kl[n, j * NT + t] = mask[j][t].astype(jnp.int32)
 
-    def read_mask(n):
-        return [[kl[n, j * NT + t] for t in range(NT)] for j in range(NJ)]
-
-    def factors(mask, k, a, b):
-        return zipped(lambda n: jnp.where(n > k + 1, a, jnp.where(n == k + 1, b, 0.0)), mask)
-
     def block(f, m, k):
-        return [[inb.at[f, m, t, k][pl.ds(j, NS, stride=NJ), :] for t in range(NT)] for j in range(NJ)]
-
-    def line(ref, m, k):
-        return [ref.at[t][pl.ds(m * NK + k, NS, stride=0), :] for t in range(NT)]
-
-    def solve(f, m, k, side_k, scale):
-        for j in range(NJ):
-            for t in range(NT):
-                i = j * NT + t
-                sbuf[f, m, k + 1, i] = (side_k[j][t] + sbuf[f, m, k, i]) * scale[j][t]
+        return [[place(f, m, t, k)[pl.ds(j, NS, stride=NJ), :] for t in range(NT)] for j in range(NJ)]
 
     def momentum(m, k, carry, wet_x, wet_y, inv_x, inv_y):
         cs, cs_n, cs_e = carry
-        uu, vv, tt, ss = (block(f, m, k) for f in range(4))
+        uu, vv, tt, ss = (block(f, m, k) for f in range(NF))
         amount = NL - 1 - m - 2 * k
-        eu, ev, et, es = ([pltpu.roll(x, amount, 1) for x in strided(ew.at[f, m])] for f in range(4))
+        eu, ev, et, es = ([pltpu.roll(x, amount, 1) for x in strided(ew.at[f, m])] for f in range(NF))
         c = pltpu.roll(corner[m], amount, 1)
         for j in range(NJ):
-            ends[0, m, k, j] = et[j]
-            ends[1, m, k, j] = es[j]
-        nu, nv, nt, ns = (line(hN.at[f], m, k) for f in range(4))
+            ends_t[m, k, j] = et[j]
+            ends_s[m, k, j] = es[j]
+        nu, nv, nt, ns = (line(hN.at[f], m, k) for f in range(NF))
         su, sv = (line(hS.at[f], m, k) for f in range(2))
 
         half = zipped(lambda s, t: PA * s - PB * t, ss, tt)
@@ -438,8 +490,8 @@
                     wet_y, p, p_n, u_sum, v_e, v_w, vv, v_n, v_s)
         bu = zipped(jnp.add, uu, gu)
         bv = zipped(jnp.add, vv, gv)
-        solve(0, m, k, bu, inv_x)
-        solve(1, m, k, bv, inv_y)
+        solve(sbuf, 0, m, k, bu, inv_x)
+        solve(sbuf, 1, m, k, bv, inv_y)
         for f, (g, b) in enumerate(((gu, bu), (gv, bv))):
             for j in range(NJ):
                 for t in range(NT):
@@ -451,7 +503,7 @@
     def momentum_levels(q, carry):
         for h in range(MOM_UNROLL):
             k = q * MOM_UNROLL + h
-            mask_x, mask_y = read_mask(1), read_mask(2)
+            mask_x, mask_y = read_mask(kl, 1), read_mask(kl, 2)
             a1, b1 = tab[0, k], tab[1, k]
             inv = factors(mask_x, k, a1, b1), factors(mask_y, k, a1, b1)
             wet_k = [zipped(lambda n: n > k, mask) for mask in (mask_x, mask_y)]
@@ -471,30 +523,7 @@
     forces = Exchange(fmain, fside, fwin, fwside, f_send, f_recv, col, row)
     forces.start()
 
-    def tracer(f, m, k, uu, vv, u_w, sv, inv_c):
-        x = block(f, m, k)
-        halo = [ends[f - 2, m, k, j] for j in range(NJ)]
-        x_e, x_w = east(x, halo), west(x, halo)
-        x_n = north(x, line(hN.at[f], m, k))
-        s_halo = line(hS.at[f], m, k)
-        fx = zipped(lambda u, a, b: u * (a + b), uu, x, x_e)
-        fx_w = zipped(lambda u, a, b: u * (a + b), u_w, x, x_w)
-        fy = zipped(lambda v, a, b: v * (a + b), vv, x, x_n)
-        fy_s = south(fy, [sv[t] * (s_halo[t] + x[0][t]) for t in range(NT)])
-        solve(f, m, k, zipped(lambda a, f, fw, g, gs: (a + a) - (f - fw) - (g - gs), x, fx, fx_w, fy, fy_s), inv_c)
-
-    def tracer_levels(q, carry):
-        for h in range(TRC_UNROLL):
-            k = q * TRC_UNROLL + h
-            inv_c = factors(read_mask(0), k, tab[2, k], tab[3, k])
-            for m in range(NM):
-                uu, vv, sv = block(0, m, k), block(1, m, k), line(hS.at[1], m, k)
-                u_w = [[uw_all[m, k, j * NT + t] for t in range(NT)] for j in range(NJ)]
-                for f in (2, 3):
-                    tracer(f, m, k, uu, vv, u_w, sv, inv_c)
-        return carry
-
-    lax.fori_loop(0, NK // TRC_UNROLL, tracer_levels, 0)
+    tracer_pass(inb, lambda m: (inb_t, (m,)), ends_t, uw_all, hN.at[2], hS.at[2], hS.at[1], kl, tab, sbuf, 2)
 
     windows.wait()
     dep = [[window_tile(main, side, 3, j, t, lane, 1, 0) for t in range(WT)] for j in range(WJ)]
@@ -538,7 +567,7 @@
                 nat.at[3, t][here, :] = 1.0 / jnp.where(ky > 0.0, hy, 1.0)
     own = pl.ds(pl.multiple_of(core * NY, NS), NY)
     for t in range(NT):
-        for i in range(4):
+        for i in range(NF):
             rl[i, t] = nat[i, t, own]
 
     def tail(i, carry):
@@ -584,7 +613,7 @@
                 state[2, n] = (state[2, n] + state[4, n]) - wi[1, n] * (en - e[t])
         return remain - w
 
-    lax.fori_loop(0, NSUB, subcycle, total)
+    lax.fori_loop(0, NSUB, subcycle, total, unroll=SUB_UNROLL)
 
     scale = 1.0 / COURANT
     for j in range(WJ):
@@ -609,6 +638,7 @@
 
 def step_call(vel_x, vel_y, pot_temp, salinity, surf_eta, trans_x, trans_y, col_depth, wet_levels, weights, tab):
     dma = pltpu.SemaphoreType.DMA
+    pair = dma((NM,))
     nreg = NJ * NT
     nwin = WJ * WT
 
@@ -618,34 +648,36 @@
     return pl.pallas_call(
         step_kernel,
         out_shape=(
-            vm(4, NM, NK + 1, nreg, *VR),
+            vm(3, NM, NK + 1, nreg, *VR),
             vm(2, NM, nreg, *VR),
             pltpu.VMEM((3, nreg, *VR), jnp.int32),
             vm(4, NT, NY, NL),
             vm(NM, 3, NT, NY, NL),
+            vm(3, NM, NT, NK, NY, NL), vm(NM, NK, NJ, *VR), vm(NM, NK, nreg, *VR), vm(4, NT, NM * NK, NL), vm(4, NT, NM * NK, NL),
         ),
-        in_specs=[ANY] * 4 + [VM] * 5 + [SM] * 2,
-        out_specs=(VM,) * 5,
+        in_specs=[HBM] * 4 + [VM] * 5 + [SM] * 2,
+        out_specs=(VM,) * 10,
         scratch_shapes=[
-            vm(4, NM, NT, NK, NY, NL),
-            vm(4, NM, NY, NL), vm(2, NM, NK, NJ, *VR), vm(NM, *VR), vm(NT, NM * NK, NL), vm(NT, NM * NK, NL), vm(NM, NK, nreg, *VR),
-            vm(4, NY, NL), vm(4, NY, NL), vm(4, NT, NM * NK, NL), vm(4, NT, NM * NK, NL), vm(*VR), vm(*VR),
-            vm(4, NY, NL), vm(4, NY, NL), vm(4, NT, NM * NK, NL), vm(4, NT, NM * NK, NL),
+            vm(NM, NT, NK, NY, NL),
+            vm(4, NM, NY, NL), vm(NM, NK, NJ, *VR), vm(NM, *VR), vm(NT, NM * NK, NL), vm(NT, NM * NK, NL),
+            vm(NF, NY, NL), vm(NF, NY, NL), vm(*VR), vm(*VR),
+            vm(NF, NY, NL), vm(NF, NY, NL), vm(NF, NT, NM * NK, NL), vm(NF, NT, NM * NK, NL),
             vm(NT, NY, NL), vm(NY, NL), vm(NT, *VR),
             vm(NM, 5, NT, NY, NL), vm(NM, 2, 2, NY, NL), vm(5, NT, WY, NL), vm(2, 2, WY, NL),
             vm(2, NM, nreg, *VR),
             vm(NM, 2, NT, NY, NL), vm(NM, 2, 1, NY, NL), vm(2, NT, WY, NL), vm(2, 1, WY, NL),
             vm(4, nwin, *VR), vm(4, NT, WY, NL), vm(7, nwin, *VR), vm(3, NT, WY, NL),
-            dma((4, NM, NT, NC)), dma((2, 4)), dma((4,)), dma((4,)), dma((2, 4)), dma((4,)), dma((4,)), dma((2,)), dma((2,)), dma((2,)), dma((2,)),
-            dma((16,)), dma((2,)), dma((16,)), dma((2,)), dma, dma, dma,
+            dma((NF, NM, NT, NC)), dma((NM, NF)), dma((NF,)), dma((NF,)), dma((NM, NF)), dma((NF,)), dma((NF,)), pair, pair, pair, pair,
+            dma((NS + NS,)), pair, dma((NS + NS,)), pair, dma, dma, dma,
         ],
-        compiler_params=pltpu.CompilerParams(collective_id=0, has_side_effects=True, vmem_limit_bytes=VMEM_LIMIT),
+        compiler_params=pltpu.CompilerParams(collective_id=0, has_side_effects=True, vmem_limit_bytes=STEP_LIMIT),
         name="ocean_step",
     )(vel_x, vel_y, pot_temp, salinity, surf_eta, trans_x, trans_y, col_depth, wet_levels, weights, tab)
 
 
-def final_kernel(sbuf, bsum, kl, rl, bo, tab, eta_out, tx_out, ty_out, u_out, v_out, temp_out, salt_out, xbuf, cor, out_sem):
+def final_kernel(sbuf, bsum, kl, rl, bo, inb, ends_s, uw_all, hN, hS, tab, eta_out, tx_out, ty_out, u_out, v_out, temp_out, salt_out, xbuf, s_salt, cor, out_sem):
     outs = (u_out, v_out, temp_out, salt_out)
+    parts = ((sbuf, 0), (sbuf, 1), (sbuf, 2), (s_salt, 0))
 
     def store(f, m, t, c):
         part = pl.ds(c * CH, CH)
@@ -688,7 +720,7 @@
                                 if f < 2:
                                     wet = kl[1 + f, i] > k
                                 for m in range(NM):
-                                    x = sbuf[f, m, k + 1, i] + g * xs[n]
+                                    x = parts[f][0][parts[f][1], m, k + 1, i] + g * xs[n]
                                     xs[n] = x
                                     n += 1
                                     xbuf.at[f, m, t, k][here, :] = jnp.where(wet, x + cor[f, m, i], 0.0) if f < 2 else x
@@ -700,27 +732,33 @@
 
         lax.fori_loop(0, NC, chunk, (zero,) * (len(fs) * NM * NJ * NT))
 
-    back((2, 3))
+    back((2,))
     back((0, 1))
+    for m in range(NM):
+        for i in range(NJ * NT):
+            s_salt[0, m, 0, i] = zero
+    tracer_pass(inb, lambda m: (inb, (2, m)), ends_s, uw_all, hN.at[3], hS.at[3], hS.at[1], kl, tab, s_salt, 0)
+    back((3,))
 
     def drain(c, _):
-        each_store(range(4), c, "wait")
+        each_store(range(NF), c, "wait")
         return 0
 
     lax.fori_loop(0, NC, drain, 0)
 
 
-def final_call(sbuf, bsum, kl, rl, bo, tab):
+def final_call(kept, tab):
     flat = jax.ShapeDtypeStruct((NM, NY, NX), F32)
     block = jax.ShapeDtypeStruct((NK, NM, NY, NX), F32)
-    held = [pltpu.with_memory_space_constraint(x, pltpu.VMEM) for x in (sbuf, bsum, kl, rl, bo)]
+    held = [pltpu.with_memory_space_constraint(x, pltpu.VMEM) for x in kept]
     return pl.pallas_call(
         final_kernel,
         out_shape=(flat,) * 3 + (block,) * 4,
-        in_specs=[VM] * 5 + [SM],
-        out_specs=(VM,) * 3 + (ANY,) * 4,
+        in_specs=[VM] * len(held) + [SM],
+        out_specs=(VM,) * 3 + (HBM,) * 4,
         scratch_shapes=[
             pltpu.VMEM((4, NM, NT, NK, NY, NL), F32),
+            pltpu.VMEM((1, NM, NK + 1, NJ * NT, *VR), F32),
             pltpu.VMEM((2, NM, NJ * NT, *VR), F32),
             pltpu.SemaphoreType.DMA((4, NM, NT, NC)),
         ],
@@ -732,8 +770,7 @@
 def solution(mesh):
     def local_step(*args):
         tab = level_table()
-        sbuf, bsum, kl, rl, bo = step_call(*args, tab)
-        return final_call(sbuf, bsum, kl, rl, bo, tab)
+        return final_call(step_call(*args, tab), tab)
 
     spec_3d = P(None, None, "row", "col")
     spec_2d = P(None, "row", "col")

time: 56.5 us -> 54.3 us (0.961)
  Pallas kernels: 55.7 us -> 53.5 us
    pallas_call x1, Pallas kernels: 47.7 us -> 43 us  [step_call(): pl.pallas_call(step_kernel, out_shape=(vm(3, NM, NK + 1, nreg, *VR), vm(2...]
    pallas_call x1, Pallas kernels: 8.04 us -> 10.5 us  [final_call(): pl.pallas_call(final_kernel, out_shape=(flat,) * 3 + (block,) * 4, in_spe...]
where the time goes in v2:
time: 54.3 us; the launch traced here: 54.2 us
  Pallas kernels  53.5 us (99%)
  between operations  0.64 us (1%)
    pallas_call x1, Pallas kernels, step_call(): pl.pallas_call(step_kernel, out_shape=(vm(3, NM, NK + 1, nreg, *VR), vm(2...  43 us
    pallas_call x1, Pallas kernels, final_call(): pl.pallas_call(final_kernel, out_shape=(flat,) * 3 + (block,) * 4, in_spe...  10.5 us

profile of v2, /device:TPU:0, one launch (start us, length us, event | category | flops | bytes accessed | tf_op | source)
XLA Modules:
  0.0 54.2 jit_solution(420578693356823434)
XLA Ops:
  0.6 43.0 %ocean_step.1 = (f32[3,2,61,8,8,128]{5,4,3,2,1,0:T(8,128)S(1)}, f32[2,2,8,8,128]{4,3,2,1,0:T(8,128)S(1)}, s32[3,8,8,128]{3,2,1,0:T(8,128)S(1)}, f32[4,2,32,128]{...) custom-call(f32[60,2,32,256]{3,2,1,0:T(8,128)} %u.1, ...), custom_call_target="tpu_custom_call" | custom-call | tf_op jit(solution)/shard_map/ocean_step/pallas_call | solution.py:648
  43.6 10.5 %back_substitution.1 = (f32[2,32,256]{2,1,0:T(8,128)}, f32[2,32,256]{2,1,0:T(8,128)}, f32[2,32,256]{2,1,0:T(8,128)}, f32[60,2,32,256]{3,2,1,0:T(8,128)}, f32[60,...) custom-call(f32[3,2,61,8,8,128]{5,4,3,2,1,0:T(8,128)S(1)} %get-tuple-element.17.sbuf, ...), custom_call_target="tpu_custom_call" | custom-call | tf_op jit(solution)/shard_map/back_substitution/pallas_call | solution.py:754

commit v3 on v2

--- a/solution.py
+++ b/solution.py
@@ -288,7 +288,7 @@
     for t in range(NT):
         ksrc[t] = wet[:, pl.ds(t * NL, NL)].astype(F32)
 
-    greet(col, row)()
+    meet = greet(col, row)
 
     def remote(s, d, ssem, rsem, dc, dr):
         return pltpu.make_async_remote_copy(src_ref=s, dst_ref=d, send_sem=ssem, recv_sem=rsem, device_id=device(dc, dr), device_id_type=MESH)
@@ -334,6 +334,7 @@
             colF[f, pl.ds(i * NS, NS)] = acc[2 * i]
             colL[f, pl.ds(i * NS, NS)] = acc[2 * i + 1]
         if f == 0:
+            meet()
             k_west.start()
 
             @pl.when(has_south)

time: 54.3 us -> 53.4 us (0.983)
  Pallas kernels: 53.5 us -> 52.6 us
    pallas_call x1, Pallas kernels: 43 us -> 42.1 us  [step_call(): pl.pallas_call(step_kernel, out_shape=(vm(3, NM, NK + 1, nreg, *VR), vm(2...]
where the time goes in v3:
time: 53.4 us; the launch traced here: 53.2 us
  Pallas kernels  52.6 us (99%)
  between operations  0.64 us (1%)
    pallas_call x1, Pallas kernels, step_call(): pl.pallas_call(step_kernel, out_shape=(vm(3, NM, NK + 1, nreg, *VR), vm(2...  42.1 us
    pallas_call x1, Pallas kernels, final_call(): pl.pallas_call(final_kernel, out_shape=(flat,) * 3 + (block,) * 4, in_spe...  10.5 us

profile of v3, /device:TPU:0, one launch (start us, length us, event | category | flops | bytes accessed | tf_op | source)
XLA Modules:
  0.0 53.2 jit_solution(4019683391484230656)
XLA Ops:
  0.6 42.1 %ocean_step.1 = (f32[3,2,61,8,8,128]{5,4,3,2,1,0:T(8,128)S(1)}, f32[2,2,8,8,128]{4,3,2,1,0:T(8,128)S(1)}, s32[3,8,8,128]{3,2,1,0:T(8,128)S(1)}, f32[4,2,32,128]{...) custom-call(f32[60,2,32,256]{3,2,1,0:T(8,128)} %u.1, ...), custom_call_target="tpu_custom_call" | custom-call | tf_op jit(solution)/shard_map/ocean_step/pallas_call | solution.py:649
  42.7 10.5 %back_substitution.1 = (f32[2,32,256]{2,1,0:T(8,128)}, f32[2,32,256]{2,1,0:T(8,128)}, f32[2,32,256]{2,1,0:T(8,128)}, f32[60,2,32,256]{3,2,1,0:T(8,128)}, f32[60,...) custom-call(f32[3,2,61,8,8,128]{5,4,3,2,1,0:T(8,128)S(1)} %get-tuple-element.17.sbuf, ...), custom_call_target="tpu_custom_call" | custom-call | tf_op jit(solution)/shard_map/back_substitution/pallas_call | solution.py:755

commit v4 on v3

--- a/solution.py
+++ b/solution.py
@@ -20,6 +20,7 @@
 NT = NX // NL
 NJ = NY // 8
 CH = 10
+HALF = CH // 2
 NC = NK // CH
 HALO = 40
 WY = 2 * NY + HALO
@@ -157,9 +158,10 @@
 
 PA = 0.15 * 0.5 / NK * 0.5
 PB = 0.2 * 0.5 / NK * 0.5
-MOM_UNROLL = 2
-TRC_UNROLL = 4
-SUB_UNROLL = 1
+MOM_UNROLL = 3
+TRC_UNROLL = 3
+BACK_UNROLL = 6
+SUB_UNROLL = 4
 
 
 def rolls(x, amount):
@@ -217,7 +219,7 @@
             sbuf[f, m, k + 1, i] = (side[j][t] + sbuf[f, m, k, i]) * scale[j][t]
 
 
-def tracer_pass(inb, field, ends, uw_all, north_rows, south_rows, south_v, kl, tab, sbuf, f):
+def tracer_pass(inb, field, ends, uw_all, north_rows, south_rows, south_v, kl, tab, sbuf, f, unroll):
     def level(m, k, inv_c):
         uu, vv, sv = read_block(inb, (0, m), k), read_block(inb, (1, m), k), line(south_v, m, k)
         u_w = [[uw_all[m, k, j * NT + t] for t in range(NT)] for j in range(NJ)]
@@ -233,14 +235,14 @@
         solve(sbuf, f, m, k, zipped(lambda a, b, bw, g, gs: (a + a) - (b - bw) - (g - gs), x, fx, fx_w, fy, fy_s), inv_c)
 
     def levels(q, carry):
-        for h in range(TRC_UNROLL):
-            k = q * TRC_UNROLL + h
+        for h in range(unroll):
+            k = q * unroll + h
             inv_c = factors(read_mask(kl, 0), k, tab[2, k], tab[3, k])
             for m in range(NM):
                 level(m, k, inv_c)
         return carry
 
-    lax.fori_loop(0, NK // TRC_UNROLL, levels, 0)
+    lax.fori_loop(0, NK // unroll, levels, 0)
 
 
 def step_kernel(u, v, temp, salt, eta, tx, ty, depth, wet, weights, tab,
@@ -313,9 +315,12 @@
     for f in range(NF):
         def chunk(c, acc, f=f):
             each_load(f, c, "wait")
+            return lax.fori_loop(0, 2, lambda h, acc: piece(c * CH + h * HALF, acc), acc)
+
+        def piece(k0, acc, f=f):
             acc = list(acc)
-            for q in range(CH):
-                k = c * CH + q
+            for q in range(HALF):
+                k = k0 + q
                 for m in range(NM):
                     spot = 2 * k + m
                     hit, hit_last = lane == spot, lane_next == spot
@@ -524,7 +529,7 @@
     forces = Exchange(fmain, fside, fwin, fwside, f_send, f_recv, col, row)
     forces.start()
 
-    tracer_pass(inb, lambda m: (inb_t, (m,)), ends_t, uw_all, hN.at[2], hS.at[2], hS.at[1], kl, tab, sbuf, 2)
+    tracer_pass(inb, lambda m: (inb_t, (m,)), ends_t, uw_all, hN.at[2], hS.at[2], hS.at[1], kl, tab, sbuf, 2, TRC_UNROLL)
 
     windows.wait()
     dep = [[window_tile(main, side, 3, j, t, lane, 1, 0) for t in range(WT)] for j in range(WJ)]
@@ -548,18 +553,17 @@
             hy = jnp.where(ky > 0.0, 0.5 * (d + dn), 0.0)
             ix = 1.0 / jnp.maximum(kx, 1.0)
             iy = 1.0 / jnp.maximum(ky, 1.0)
-            n = j * WT + t
-            state[0, n] = window_tile(main, side, 0, j, t, lane, 0, 0)
+            state[0, j, t] = window_tile(main, side, 0, j, t, lane, 0, 0)
             for i in (1, 2):
                 first = COURANT * window_tile(main, side, i, j, t, lane, 0, i)
-                state[i, n] = first
-                wi[1 + i, n] = first
-            wi[0, n] = (COURANT * COURANT) * hx
-            wi[1, n] = (COURANT * COURANT) * hy
-            state[3, n] = (COURANT / NSUB) * hx * ix
-            state[4, n] = (COURANT / NSUB) * hy * iy
-            state[5, n] = zero
-            state[6, n] = zero
+                state[i, j, t] = first
+                wi[1 + i, j, t] = first
+            wi[0, j, t] = (COURANT * COURANT) * hx
+            wi[1, j, t] = (COURANT * COURANT) * hy
+            state[3, j, t] = (COURANT / NSUB) * hx * ix
+            state[4, j, t] = (COURANT / NSUB) * hy * iy
+            state[5, j, t] = zero
+            state[6, j, t] = zero
             if t < NT:
                 here = pl.ds(j, NS, stride=WJ)
                 nat.at[0, t][here, :] = ix
@@ -581,53 +585,45 @@
     forces.wait()
     for j in range(WJ):
         for t in range(WT):
-            n = j * WT + t
             for f in range(2):
-                state[3 + f, n] = state[3 + f, n] * window_tile(fwin, fwside, f, j, t, lane, 0, f)
+                state[3 + f, j, t] = state[3 + f, j, t] * window_tile(fwin, fwside, f, j, t, lane, 0, f)
+
+    lane3 = lax.broadcasted_iota(jnp.int32, (WT, *VR), 2)
+    wall3 = jnp.broadcast_to(edge_wall, (WT, *VR))
 
     def subcycle(i, remain):
         w = weights[i]
         for j in range(WJ):
-            r = [pltpu.roll(state[1, j * WT + t], 1, 1) for t in range(WT)]
-            for t in range(WT):
-                n = j * WT + t
-                uw = jnp.where(l_first, r[(t + WT - 1) % WT], r[t])
-                if j == 0:
-                    vs = pltpu.roll(state[2, (WJ - 1) * WT + t], 1, 0) * edge_wall
-                else:
-                    vs = state[2, n - WT]
-                e = state[0, n] - ((state[1, n] - uw) + (state[2, n] - vs))
-                state[0, n] = e
-                state[5, n] = state[5, n] + w * e
-                state[6, n] = state[6, n] + remain * e
+            u, v = state[1, j], state[2, j]
+            r = pltpu.roll(u, 1, 2)
+            uw = jnp.where(lane3 == 0, jnp.concatenate([r[WT - 1:], r[:WT - 1]], axis=0), r)
+            vs = state[2, j - 1] if j else pltpu.roll(state[2, WJ - 1], 1, 1) * wall3
+            e = state[0, j] - ((u - uw) + (v - vs))
+            state[0, j] = e
+            state[5, j] = state[5, j] + w * e
+            state[6, j] = state[6, j] + remain * e
         for j in range(WJ):
-            e = [state[0, j * WT + t] for t in range(WT)]
-            r = [pltpu.roll(e[t], NL - 1, 1) for t in range(WT)]
-            for t in range(WT):
-                n = j * WT + t
-                ee = jnp.where(l_last, r[(t + 1) % WT], r[t])
-                if j == WJ - 1:
-                    en = pltpu.roll(state[0, t], NS - 1, 0)
-                else:
-                    en = state[0, n + WT]
-                state[1, n] = (state[1, n] + state[3, n]) - wi[0, n] * (ee - e[t])
-                state[2, n] = (state[2, n] + state[4, n]) - wi[1, n] * (en - e[t])
+            e = state[0, j]
+            r = pltpu.roll(e, NL - 1, 2)
+            ee = jnp.where(lane3 == NL - 1, jnp.concatenate([r[1:], r[:1]], axis=0), r)
+            en = state[0, j + 1] if j < WJ - 1 else pltpu.roll(state[0, 0], NS - 1, 1)
+            state[1, j] = (state[1, j] + state[3, j]) - wi[0, j] * (ee - e)
+            state[2, j] = (state[2, j] + state[4, j]) - wi[1, j] * (en - e)
         return remain - w
 
     lax.fori_loop(0, NSUB, subcycle, total, unroll=SUB_UNROLL)
 
     scale = 1.0 / COURANT
     for j in range(WJ):
-        q = [state[6, j * WT + t] for t in range(WT)]
+        q = [state[6, j, t] for t in range(WT)]
         r = [pltpu.roll(q[t], NL - 1, 1) for t in range(WT)]
         for t in range(NT):
-            n = j * WT + t
             qe = jnp.where(l_last, r[t + 1], r[t])
-            qn = pltpu.roll(state[6, t], NS - 1, 0) if j == WJ - 1 else state[6, n + WT]
+            qn = pltpu.roll(state[6, 0, t], NS - 1, 0) if j == WJ - 1 else state[6, j + 1, t]
             here = pl.ds(j, NS, stride=WJ)
-            res.at[0, t][here, :] = state[5, n]
-            res.at[1, t][here, :] = scale * (total * wi[2, n] + moment * state[3, n] - wi[0, n] * (qe - q[t]))
-            res.at[2, t][here, :] = scale * (total * wi[3, n] + moment * state[4, n] - wi[1, n] * (qn - q[t]))
+            res.at[0, t][here, :] = state[5, j, t]
+            res.at[1, t][here, :] = scale * (total * wi[2, j, t] + moment * state[3, j, t] - wi[0, j, t] * (qe - q[t]))
+            res.at[2, t][here, :] = scale * (total * wi[3, j, t] + moment * state[4, j, t] - wi[1, j, t] * (qn - q[t]))
     other = 1 - core
     send = remote(res.at[:, :, pl.ds(pl.multiple_of(other * NY, NS), NY)], out.at[core], out_send, out_recv, col, chip * 2 + other)
     send.start()
@@ -641,7 +637,6 @@
     dma = pltpu.SemaphoreType.DMA
     pair = dma((NM,))
     nreg = NJ * NT
-    nwin = WJ * WT
 
     def vm(*shape):
         return pltpu.VMEM(shape, F32)
@@ -667,7 +662,7 @@
             vm(NM, 5, NT, NY, NL), vm(NM, 2, 2, NY, NL), vm(5, NT, WY, NL), vm(2, 2, WY, NL),
             vm(2, NM, nreg, *VR),
             vm(NM, 2, NT, NY, NL), vm(NM, 2, 1, NY, NL), vm(2, NT, WY, NL), vm(2, 1, WY, NL),
-            vm(4, nwin, *VR), vm(4, NT, WY, NL), vm(7, nwin, *VR), vm(3, NT, WY, NL),
+            vm(4, WJ, WT, *VR), vm(4, NT, WY, NL), vm(7, WJ, WT, *VR), vm(3, NT, WY, NL),
             dma((NF, NM, NT, NC)), dma((NM, NF)), dma((NF,)), dma((NF,)), dma((NM, NF)), dma((NF,)), dma((NF,)), pair, pair, pair, pair,
             dma((NS + NS,)), pair, dma((NS + NS,)), pair, dma, dma, dma,
         ],
@@ -738,7 +733,7 @@
     for m in range(NM):
         for i in range(NJ * NT):
             s_salt[0, m, 0, i] = zero
-    tracer_pass(inb, lambda m: (inb, (2, m)), ends_s, uw_all, hN.at[3], hS.at[3], hS.at[1], kl, tab, s_salt, 0)
+    tracer_pass(inb, lambda m: (inb, (2, m)), ends_s, uw_all, hN.at[3], hS.at[3], hS.at[1], kl, tab, s_salt, 0, BACK_UNROLL)
     back((3,))
 
     def drain(c, _):

time: 53.4 us -> 51.4 us (0.963)
  Pallas kernels: 52.6 us -> 50.5 us
    pallas_call x1, Pallas kernels: 42.1 us -> 40.3 us  [step_call(): pl.pallas_call(step_kernel, out_shape=(vm(3, NM, NK + 1, nreg, *VR), vm(2...]
where the time goes in v4:
time: 51.4 us; the launch traced here: 51.2 us
  Pallas kernels  50.5 us (98%)
  between operations  0.64 us (1%)
    pallas_call x1, Pallas kernels, step_call(): pl.pallas_call(step_kernel, out_shape=(vm(3, NM, NK + 1, nreg, *VR), vm(2...  40.3 us
    pallas_call x1, Pallas kernels, final_call(): pl.pallas_call(final_kernel, out_shape=(flat,) * 3 + (block,) * 4, in_spe...  10.3 us

profile of v4, /device:TPU:0, one launch (start us, length us, event | category | flops | bytes accessed | tf_op | source)
XLA Modules:
  0.0 51.2 jit_solution(16506504936132689524)
XLA Ops:
  0.6 40.3 %ocean_step.1 = (f32[3,2,61,8,8,128]{5,4,3,2,1,0:T(8,128)S(1)}, f32[2,2,8,8,128]{4,3,2,1,0:T(8,128)S(1)}, s32[3,8,8,128]{3,2,1,0:T(8,128)S(1)}, f32[4,2,32,128]{...) custom-call(f32[60,2,32,256]{3,2,1,0:T(8,128)} %u.1, ...), custom_call_target="tpu_custom_call" | custom-call | tf_op jit(solution)/shard_map/ocean_step/pallas_call | solution.py:644
  40.9 10.3 %back_substitution.1 = (f32[2,32,256]{2,1,0:T(8,128)}, f32[2,32,256]{2,1,0:T(8,128)}, f32[2,32,256]{2,1,0:T(8,128)}, f32[60,2,32,256]{3,2,1,0:T(8,128)}, f32[60,...) custom-call(f32[3,2,61,8,8,128]{5,4,3,2,1,0:T(8,128)S(1)} %get-tuple-element.17.sbuf, ...), custom_call_target="tpu_custom_call" | custom-call | tf_op jit(solution)/shard_map/back_substitution/pallas_call | solution.py:750

commit v5 on v4

--- a/solution.py
+++ b/solution.py
@@ -20,7 +20,7 @@
 NT = NX // NL
 NJ = NY // 8
 CH = 10
-HALF = CH // 2
+HALF = CH
 NC = NK // CH
 HALO = 40
 WY = 2 * NY + HALO
@@ -315,7 +315,7 @@
     for f in range(NF):
         def chunk(c, acc, f=f):
             each_load(f, c, "wait")
-            return lax.fori_loop(0, 2, lambda h, acc: piece(c * CH + h * HALF, acc), acc)
+            return piece(c * CH, acc)
 
         def piece(k0, acc, f=f):
             acc = list(acc)
@@ -375,7 +375,6 @@
         pack_side(wside, m, 0, reads[:3], lane)
         pack_side(wside, m, 1, reads[3:], lane)
     windows = Exchange(wmain, wside, main, side, w_send, w_recv, col, row)
-    windows.start()
 
     @pl.when(jnp.logical_not(has_north))
     def _():
@@ -517,6 +516,7 @@
         return carry
 
     start = ([[zero] * NT for _ in range(NJ)], [zero] * NT, [zero] * NJ)
+    windows.start()
     lax.fori_loop(0, NK // MOM_UNROLL, momentum_levels, (start, start))
 
     for f in range(2):

time: 51.4 us -> 49.9 us (0.971)
  Pallas kernels: 50.5 us -> 49.1 us
    pallas_call x1, Pallas kernels: 40.3 us -> 38.8 us  [step_call(): pl.pallas_call(step_kernel, out_shape=(vm(3, NM, NK + 1, nreg, *VR), vm(2...]
where the time goes in v5:
time: 49.9 us; the launch traced here: 49.8 us
  Pallas kernels  49.1 us (98%)
  between operations  0.64 us (1%)
    pallas_call x1, Pallas kernels, step_call(): pl.pallas_call(step_kernel, out_shape=(vm(3, NM, NK + 1, nreg, *VR), vm(2...  38.8 us
    pallas_call x1, Pallas kernels, final_call(): pl.pallas_call(final_kernel, out_shape=(flat,) * 3 + (block,) * 4, in_spe...  10.3 us

profile of v5, /device:TPU:0, one launch (start us, length us, event | category | flops | bytes accessed | tf_op | source)
XLA Modules:
  0.0 49.8 jit_solution(13708965581363016078)
XLA Ops:
  0.6 38.8 %ocean_step.1 = (f32[3,2,61,8,8,128]{5,4,3,2,1,0:T(8,128)S(1)}, f32[2,2,8,8,128]{4,3,2,1,0:T(8,128)S(1)}, s32[3,8,8,128]{3,2,1,0:T(8,128)S(1)}, f32[4,2,32,128]{...) custom-call(f32[60,2,32,256]{3,2,1,0:T(8,128)} %u.1, ...), custom_call_target="tpu_custom_call" | custom-call | tf_op jit(solution)/shard_map/ocean_step/pallas_call | solution.py:644
  39.5 10.3 %back_substitution.1 = (f32[2,32,256]{2,1,0:T(8,128)}, f32[2,32,256]{2,1,0:T(8,128)}, f32[2,32,256]{2,1,0:T(8,128)}, f32[60,2,32,256]{3,2,1,0:T(8,128)}, f32[60,...) custom-call(f32[3,2,61,8,8,128]{5,4,3,2,1,0:T(8,128)S(1)} %get-tuple-element.17.sbuf, ...), custom_call_target="tpu_custom_call" | custom-call | tf_op jit(solution)/shard_map/back_substitution/pallas_call | solution.py:750

commit v6 on v5

--- a/solution.py
+++ b/solution.py
@@ -160,8 +160,8 @@
 PB = 0.2 * 0.5 / NK * 0.5
 MOM_UNROLL = 3
 TRC_UNROLL = 3
-BACK_UNROLL = 6
-SUB_UNROLL = 4
+BACK_UNROLL = 10
+SUB_UNROLL = 5
 
 
 def rolls(x, amount):

time: 49.9 us -> 49.6 us (level)
  no operation moved by 1% of the time
where the time goes in v6:
time: 49.6 us; the launch traced here: 49.4 us
  Pallas kernels  48.8 us (98%)
  between operations  0.64 us (1%)
    pallas_call x1, Pallas kernels, step_call(): pl.pallas_call(step_kernel, out_shape=(vm(3, NM, NK + 1, nreg, *VR), vm(2...  38.7 us
    pallas_call x1, Pallas kernels, final_call(): pl.pallas_call(final_kernel, out_shape=(flat,) * 3 + (block,) * 4, in_spe...  10 us

profile of v6, /device:TPU:0, one launch (start us, length us, event | category | flops | bytes accessed | tf_op | source)
XLA Modules:
  0.0 49.4 jit_solution(15375363811397636347)
XLA Ops:
  0.6 38.7 %ocean_step.1 = (f32[3,2,61,8,8,128]{5,4,3,2,1,0:T(8,128)S(1)}, f32[2,2,8,8,128]{4,3,2,1,0:T(8,128)S(1)}, s32[3,8,8,128]{3,2,1,0:T(8,128)S(1)}, f32[4,2,32,128]{...) custom-call(f32[60,2,32,256]{3,2,1,0:T(8,128)} %u.1, ...), custom_call_target="tpu_custom_call" | custom-call | tf_op jit(solution)/shard_map/ocean_step/pallas_call | solution.py:644
  39.4 10.0 %back_substitution.1 = (f32[2,32,256]{2,1,0:T(8,128)}, f32[2,32,256]{2,1,0:T(8,128)}, f32[2,32,256]{2,1,0:T(8,128)}, f32[60,2,32,256]{3,2,1,0:T(8,128)}, f32[60,...) custom-call(f32[3,2,61,8,8,128]{5,4,3,2,1,0:T(8,128)S(1)} %get-tuple-element.17.sbuf, ...), custom_call_target="tpu_custom_call" | custom-call | tf_op jit(solution)/shard_map/back_substitution/pallas_call | solution.py:750

commit v7 on v6

--- a/solution.py
+++ b/solution.py
@@ -21,6 +21,7 @@
 NJ = NY // 8
 CH = 10
 HALF = CH
+GROUP = 5
 NC = NK // CH
 HALO = 40
 WY = 2 * NY + HALO
@@ -704,8 +705,8 @@
 
             def step(q, xs):
                 xs = list(xs)
-                for h in range(2):
-                    k = c * CH + CH - 1 - 2 * q - h
+                for h in range(GROUP):
+                    k = c * CH + CH - 1 - GROUP * q - h
                     n = 0
                     for f in fs:
                         g = tab[f // 2 * 2, k]
@@ -722,7 +723,7 @@
                                     xbuf.at[f, m, t, k][here, :] = jnp.where(wet, x + cor[f, m, i], 0.0) if f < 2 else x
                 return tuple(xs)
 
-            xs = lax.fori_loop(0, CH // 2, step, xs)
+            xs = lax.fori_loop(0, CH // GROUP, step, xs)
             each_store(fs, c, "start")
             return xs
 

time: 49.6 us -> 49.4 us (level)
  no operation moved by 1% of the time
where the time goes in v7:
time: 49.4 us; the launch traced here: 49.2 us
  Pallas kernels  48.6 us (98%)
  between operations  0.64 us (1%)
    pallas_call x1, Pallas kernels, step_call(): pl.pallas_call(step_kernel, out_shape=(vm(3, NM, NK + 1, nreg, *VR), vm(2...  38.7 us
    pallas_call x1, Pallas kernels, final_call(): pl.pallas_call(final_kernel, out_shape=(flat,) * 3 + (block,) * 4, in_spe...  9.87 us

profile of v7, /device:TPU:0, one launch (start us, length us, event | category | flops | bytes accessed | tf_op | source)
XLA Modules:
  0.0 49.2 jit_solution(17577520441986855483)
XLA Ops:
  0.6 38.7 %ocean_step.1 = (f32[3,2,61,8,8,128]{5,4,3,2,1,0:T(8,128)S(1)}, f32[2,2,8,8,128]{4,3,2,1,0:T(8,128)S(1)}, s32[3,8,8,128]{3,2,1,0:T(8,128)S(1)}, f32[4,2,32,128]{...) custom-call(f32[60,2,32,256]{3,2,1,0:T(8,128)} %u.1, ...), custom_call_target="tpu_custom_call" | custom-call | tf_op jit(solution)/shard_map/ocean_step/pallas_call | solution.py:645
  39.4 9.9 %back_substitution.1 = (f32[2,32,256]{2,1,0:T(8,128)}, f32[2,32,256]{2,1,0:T(8,128)}, f32[2,32,256]{2,1,0:T(8,128)}, f32[60,2,32,256]{3,2,1,0:T(8,128)}, f32[60,...) custom-call(f32[3,2,61,8,8,128]{5,4,3,2,1,0:T(8,128)S(1)} %get-tuple-element.17.sbuf, ...), custom_call_target="tpu_custom_call" | custom-call | tf_op jit(solution)/shard_map/back_substitution/pallas_call | solution.py:751
